TPU v7x, 256 devices: a whole 4x4x8 slice. The times are simulated.
256 devices in a mesh: model: 32 (over z, y), data: 8 (over x, core).
Axes of the slice: x: 4, y: 4, z: 8, core: 2. Of those that a mesh axis runs over, the one named last changes fastest.
Arguments:
- tokens: bfloat16 [16384, 1024], P('data')
- w_up: bfloat16 [1024, 16384], P(None, 'model')
- w_down: bfloat16 [16384, 1024], P('model')
- task_heads: bfloat16 [4, 1024, 3], replicated
- labels: int32 [4, 16384], P(None, 'data')
Outputs:
- output 1: float32 [4], replicated
- output 2: float32 [1024, 16384], P('data', 'model')
- output 3: float32 [16384, 1024], P(('model', 'data'))
All inputs are finite; a program needn't handle non-finite values.
Results may differ from a plain program's by a relative error of at most 0.001.
Values are sent between devices in bfloat16 or wider.
A program may use at most 768 MiB of HBM per device.

v0:
```python
import jax
import jax.numpy as jnp
from jax import lax
from jax.sharding import PartitionSpec as P

STEPS = 20


def simplex_weights(gram_mat):
    n_task = gram_mat.shape[0]
    trace_scale = jnp.trace(gram_mat) / n_task

    def eg_step(step_idx, weights):
        updated = weights * jnp.exp(-jnp.sum(gram_mat * weights[None, :], axis=1) / trace_scale)
        return updated / jnp.sum(updated)

    return lax.fori_loop(0, STEPS, eg_step, jnp.full((n_task,), 1.0 / n_task, jnp.float32))


def solution(mesh):
    n_data = mesh.shape['data']

    def local_step(tokens, w_up, w_down, task_heads, labels):
        n_total = tokens.shape[0] * n_data
        n_class = task_heads.shape[2]
        pre_act = jnp.dot(tokens, w_up, preferred_element_type=jnp.float32)
        act_val, gelu_slope = jax.jvp(jax.nn.gelu, (pre_act,), (jnp.ones_like(pre_act),))
        act_bf = act_val.astype(jnp.bfloat16)
        part_out = jnp.dot(act_bf, w_down, preferred_element_type=jnp.float32)
        mlp_out = lax.psum(part_out, 'model')
        trunk_out = (tokens.astype(jnp.float32) + mlp_out).astype(jnp.bfloat16)
        logits = jnp.einsum('bd,tdc->tbc', trunk_out, task_heads, preferred_element_type=jnp.float32)
        class_prob = jax.nn.softmax(logits, axis=-1)
        onehot = jax.nn.one_hot(labels, n_class, dtype=jnp.float32)
        dlogit = (class_prob - onehot) / n_total
        d_trunk = jnp.einsum('tbc,tdc->tbd', dlogit, task_heads.astype(jnp.float32), precision=lax.Precision.HIGHEST).astype(jnp.bfloat16)
        g_down = jnp.einsum('bf,tbd->tfd', act_bf, d_trunk, preferred_element_type=jnp.float32)
        d_act = jnp.einsum('tbd,fd->tbf', d_trunk, w_down, preferred_element_type=jnp.float32)
        d_pre = (d_act * gelu_slope[None]).astype(jnp.bfloat16)
        g_up = jnp.einsum('bd,tbf->tdf', tokens, d_pre, preferred_element_type=jnp.float32)
        up_shard = lax.psum_scatter(g_up, 'data', scatter_dimension=1, tiled=True)
        down_shard = lax.psum_scatter(g_down, 'data', scatter_dimension=1, tiled=True)
        gram_part = (jnp.einsum('tij,sij->ts', up_shard, up_shard, precision=lax.Precision.HIGHEST)
                     + jnp.einsum('tij,sij->ts', down_shard, down_shard, precision=lax.Precision.HIGHEST))
        gram_mat = lax.psum(gram_part, ('model', 'data'))
        task_weights = simplex_weights(gram_mat)
        grad_up = jnp.einsum('t,tij->ij', task_weights, up_shard, precision=lax.Precision.HIGHEST)
        grad_down = jnp.einsum('t,tij->ij', task_weights, down_shard, precision=lax.Precision.HIGHEST)
        return task_weights, grad_up, grad_down

    return jax.shard_map(
        local_step, mesh=mesh,
        in_specs=(P('data', None), P(None, 'model'), P('model', None), P(None, None, None), P(None, 'data')),
        out_specs=(P(None), P('data', 'model'), P(('model', 'data'), None)),
        check_vma=False)
```

profile of v0, /device:TPU:1, one launch (start us, length us, event | category | flops | bytes accessed | tf_op | source)
XLA Modules:
  0.0 582.0 jit_solution(2650401833977416654)
XLA Ops:
  7.2 8.9 %fusion.13 = (f32[2048,512]{1,0:T(8,128)}, f32[2048,512]{1,0:T(8,128)S(1)}) fusion(bf16[2048,1024]{1,0:T(8,128)(2,1)} %param.7, bf16[1024,512]{1,0:T(8,128)(2,1)} %param.8), kind=kOutput, calls=%fused_computation.21 | convolution fusion | flops 2164260864 | bytes 13631488 | tf_op jit(solution)/shard_map/dot_general | solution.py:26
  16.1 2.0 copy-done.6
  18.1 5.9 %fusion.40 = f32[2048,1024]{1,0:T(8,128)} fusion(bf16[512,1024]{1,0:T(8,128)(2,1)S(1)} %copy-done, f32[2048,512]{1,0:T(8,128)S(1)} %get-tuple-element.54), kind=kOutput, calls=%fused_computation.53 | convolution fusion | flops 2156920832 | bytes 13631488 | tf_op jit(solution)/shard_map/dot_general | solution.py:29
  24.6 214.6 %all-reduce.4.cloned.1.call-done = f32[2048,1024]{1,0:T(8,128)} async-done(((f32[2048,1024]{1,0:T(8,128)}), f32[2048,1024]{1,0:T(8,128)}) %all-reduce.4.cloned.1.call-update) | async-done | bytes 8388624 | tf_op jit(solution)/shard_map/psum | solution.py:30
  239.3 5.8 fusion.42
  245.2 14.1 %convolution_convert_fusion = bf16[4,2048,1024]{2,1,0:T(8,128)(2,1)S(1)} fusion(f32[4,2048,3]{1,0,2:T(4,128)S(1)} %fusion.32, bf16[4,1024,3]{1,0,2:T(4,128)(2,1)S(1)} %copy-done.2), kind=kOutput, calls=%fused_computation.5 | convolution fusion | flops 310378496 | bytes 16900096 | tf_op jit(solution)/shard_map/tbc,tdc->tbd/dot_general | solution.py:36
  259.3 5.7 copy-done.1
  265.0 15.2 %convolution_bitcast_fusion = f32[4,512,1024]{1,2,0:T(8,128)} fusion(bf16[4,2048,1024]{2,1,0:T(8,128)(2,1)S(1)} %convolution_convert_fusion, f32[2048,512]{1,0:T(8,128)} %copy-done.6), kind=kOutput, calls=%fused_computation.27 | convolution fusion | flops 8599371776 | bytes 29360128 | tf_op jit(solution)/shard_map/bf,tbd->tfd/dot_general | solution.py:37
  280.2 10.4 %copy.22 = f32[4,512,1024]{2,0,1:T(4,128)} copy(f32[4,512,1024]{1,2,0:T(8,128)} %convolution_bitcast_fusion) | data formatting | bytes 16777216 | tf_op jit(solution)/shard_map/bf,tbd->tfd/transpose | solution.py:37
  290.8 5.4 copy.18
  296.2 25.6 %fusion.18 = f32[4,1024,512]{1,2,0:T(8,128)} fusion(bf16[2048,1024]{1,0:T(8,128)(2,1)} %param.7, f32[2048,512]{0,1:T(8,128)} %copy.18, bf16[4,2048,1024]{2,1,0:T(8,128)(2,1)} %copy-done.1, bf16[512,1024]{1,0:T(8,128)(2,1)S(1)} %copy-done), kind=kOutput, calls=%fused_computation.26 | convolution fusion | flops 17188257792 | bytes 34603008 | tf_op jit(solution)/shard_map/bd,tbf->tdf/dot_general | solution.py:40
  321.9 0.6 copy-done.5
  323.8 74.7 %all-reduce.6.cloned.1.call-done = f32[4,512,1024]{2,0,1:T(4,128)} async-done(((f32[4,512,1024]{2,0,1:T(4,128)}), f32[4,512,1024]{2,0,1:T(4,128)}) %all-reduce.6.cloned.1.call-update) | async-done | bytes 8388624
  398.5 6.5 %convolution_bitcast_fusion.1 = f32[4,4]{1,0:T(4,128)S(1)} fusion(f32[4,512,1024]{2,0,1:T(4,128)} %all-reduce.6.cloned.1.call-done, u32[]{:T(128)S(6)} %multiply.5), kind=kOutput, calls=%fused_computation.30 | convolution fusion | flops 12582912 | bytes 1048644 | tf_op jit(solution)/shard_map/tij,sij->ts/dot_general | solution.py:44
  405.1 50.8 %reduce-scatter.2.cloned.1.call-done = f32[4,128,512]{1,2,0:T(8,128)} async-done(((f32[4,1024,512]{1,2,0:T(8,128)}), f32[4,128,512]{1,2,0:T(8,128)}) %reduce-scatter.2.cloned.1.call-update) | async-done | bytes 1048592 | tf_op jit(solution)/shard_map/reduce_scatter | solution.py:41
  455.9 1.7 copy.19
  457.6 4.9 fusion.25
  462.6 76.7 %psum.15 = f32[4,4]{1,0:T(4,128)S(1)} all-reduce(f32[4,4]{1,0:T(4,128)S(1)} %fusion.25), channel_id=1, replica_groups=mesh['model'=32,'data'=8] {'model','data'}, use_global_device_ids=true, to_apply=%region_5.6 | all-reduce | flops 16 | bytes 128 | tf_op jit(solution)/shard_map/psum | solution.py:45
  539.3 0.6 select_reduce_fusion
  540.5 28.4 %while.11 = (s32[]{:T(128)}, f32[4]{0:T(128)S(1)}, f32[4,4]{1,0:T(4,128)S(1)}, f32[]{:T(128)}, s32[]{:T(128)}, /*index=5*/s32[]{:T(128)}) while((s32[]{:T(128)}, f32[4]{0:T(128)S(1)}, f32[4,4]{1,0:T(4,128)S(1)}, f32[]{:T(128)}, s32[]{:T(128)}, /*index=5*/s32[]{:T(128)}) %tuple.31), condition=%wide.region_10.11_spmd.clone, body=%wide.region_7.10_spmd.clone.sunk | while | flops 58 | bytes 300 | solution.py:17
  540.6 0.6 fusion.53
  541.3 0.6 broadcast_divide_fusion.2
  542.1 0.6 fusion.53
  542.7 0.6 broadcast_divide_fusion.2
  543.5 0.6 fusion.53
  544.1 0.6 broadcast_divide_fusion.2
  544.9 0.6 fusion.53
  545.5 0.6 broadcast_divide_fusion.2
  546.3 0.6 fusion.53
  546.9 0.6 broadcast_divide_fusion.2
  547.7 0.6 fusion.53
  548.4 0.6 broadcast_divide_fusion.2
  549.2 0.6 fusion.53
  549.8 0.6 broadcast_divide_fusion.2
  550.6 0.6 fusion.53
  551.2 0.6 broadcast_divide_fusion.2
  552.0 0.6 fusion.53
  552.6 0.6 broadcast_divide_fusion.2
  553.4 0.6 fusion.53
  554.0 0.6 broadcast_divide_fusion.2
  554.8 0.6 fusion.53
  555.5 0.6 broadcast_divide_fusion.2
  556.3 0.6 fusion.53
  556.9 0.6 broadcast_divide_fusion.2
  557.7 0.6 fusion.53
  558.3 0.6 broadcast_divide_fusion.2
  559.1 0.6 fusion.53
  559.7 0.6 broadcast_divide_fusion.2
  560.5 0.6 fusion.53
  561.1 0.6 broadcast_divide_fusion.2
  561.9 0.6 fusion.53
  562.6 0.6 broadcast_divide_fusion.2
  563.4 0.6 fusion.53
  564.0 0.6 broadcast_divide_fusion.2
  564.8 0.6 fusion.53
  565.4 0.6 broadcast_divide_fusion.2
  566.2 0.6 fusion.53
  566.8 0.6 broadcast_divide_fusion.2
  567.6 0.6 fusion.53
  568.2 0.6 broadcast_divide_fusion.2
  568.9 1.8 fusion.38
  570.7 0.7 copy.33
  571.4 3.0 fusion.28
  574.5 0.8 copy.32
  (61 shorter events, 4.0 us)
Async XLA Ops:
  7.2 10.9 %copy-start = (bf16[512,1024]{1,0:T(8,128)(2,1)S(1)}, bf16[512,1024]{1,0:T(8,128)(2,1)}, u32[]{:S(2)}) copy-start(bf16[512,1024]{1,0:T(8,128)(2,1)} %param.9) | copy-start | bytes 3145732
  7.2 232.1 %all-reduce.4.cloned.1.call-start = ((), (), s32[]{:S(2)}) async-start(), calls=%async_computation.1 | async-start | bytes 16777216 | tf_op jit(solution)/shard_map/psum | solution.py:30
  16.1 2.0 copy-start.6
  24.0 215.3 %copy-start.2 = (bf16[4,1024,3]{1,0,2:T(4,128)(2,1)S(1)}, bf16[4,1024,3]{1,0,2:T(4,128)(2,1)}, u32[]{:S(2)}) copy-start(bf16[4,1024,3]{1,0,2:T(4,128)(2,1)} %param.10) | copy-start | bytes 73732
  24.0 221.1 %copy-start.3 = (s32[4,2048]{1,0:T(4,128)S(1)}, s32[4,2048]{1,0:T(4,128)}, u32[]{:S(2)}) copy-start(s32[4,2048]{1,0:T(4,128)} %param.11) | copy-start | bytes 98308
  24.0 374.5 %all-reduce.6.cloned.1.call-start = ((), (), s32[]{:S(2)}) async-start(), calls=%async_computation.3 | async-start | bytes 16777216
  259.3 5.7 copy-start.1
  290.6 165.3 %reduce-scatter.2.cloned.1.call-start = ((), (), s32[]{:S(2)}) async-start(), calls=%async_computation.2 | async-start | bytes 9437184 | tf_op jit(solution)/shard_map/reduce_scatter | solution.py:41
  321.9 0.7 copy-start.5
  568.9 6.3 %copy-start.4 = (f32[4]{0:T(128)}, f32[4]{0:T(128)S(1)}, u32[]{:S(2)}) copy-start(f32[4]{0:T(128)S(1)} %get-tuple-element.22) | copy-start | bytes 52
Sparse Core Ops, SparseCore 0:
  24.2 215.0 all-reduce.3
  290.7 107.7 all-reduce.5
  401.1 54.7 reduce-scatter.1
where the time goes:
time: 588 us; the launch traced here: 582 us
  waiting for transfers between devices  340 us (58%)
  matrix products  91.8 us (16%)
  blocking collectives  76.7 us (13%)
  other arithmetic  28.4 us (5%)
  local copies, waits for them, and re-layouts  27.9 us (5%)
  between operations  15.5 us (3%)
    psum x1, waiting for transfers between devices, local_step(): mlp_out = lax.psum(part_out, 'model')  215 us
    psum x1, blocking collectives, local_step(): gram_mat = lax.psum(gram_part, ('model', 'data'))  76.7 us
    unnamed x4, waiting for transfers between devices  74.8 us
    reduce_scatter x1, waiting for transfers between devices, local_step(): up_shard = lax.psum_scatter(g_up, 'data', scatter_dimension=1, tiled=True)  50.8 us
    dot_general x1, matrix products, local_step(): jnp.einsum('bd,tbf->tdf', tokens, d_pre, preferred_element_type=jnp.float32)  25.6 us
    dot_general x1, matrix products, local_step(): jnp.einsum('bf,tbd->tfd', act_bf, d_trunk, preferred_element_type=jnp.flo...  15.2 us
    dot_general x1, matrix products, local_step(): jnp.einsum('tbc,tdc->tbd', dlogit, task_heads.astype(jnp.float32), precis...  14.1 us
    div x20, other arithmetic, eg_step(): return updated / jnp.sum(updated)  13 us
  transfers between devices with their start and end apart: 3, of which 3 were waited for; matrix products, arithmetic and copies ran while one was open for 7% of the time, Pallas kernels for 0%

commit v1 on v0

v1 whole, which is shorter than its diff:
```python
import functools

import jax
import jax.numpy as jnp
import numpy as np
from jax import lax
from jax.experimental import pallas as pl
from jax.experimental.pallas import tpu as pltpu
from jax.sharding import PartitionSpec as P

STEPS = 20
NY = 4
CORES = 2
F32 = jnp.float32
BF16 = jnp.bfloat16
VMEM_LIMIT = 67043328


def chain(n):
    return [(i % 2 == 0, n // 2 - (i + 1) // 2) for i in range(n - 1)]


class Ring:
    def __init__(self, n, me, peer, chunk, recv, send_sem, recv_sem, add):
        self.n, self.me, self.peer, self.chunk = n, me, peer, chunk
        self.recv, self.send_sem, self.recv_sem, self.add = recv, send_sem, recv_sem, add
        self.order = chain(n)

    def copy(self, d, i):
        far, dist = self.order[i]
        sign = 1 if d == 0 else -1
        half = d if far else 1 - d
        dest = lax.rem(self.me + self.n + sign * dist, self.n)
        target = lax.rem(self.me + self.n + sign, self.n)
        return pltpu.make_async_remote_copy(
            src_ref=self.chunk(dest, half), dst_ref=self.recv.at[d, i],
            send_sem=self.send_sem.at[d, i], recv_sem=self.recv_sem.at[d, i],
            device_id=self.peer(target), device_id_type=pl.DeviceIdType.MESH)

    def send(self, d, i):
        self.copy(d, i).start()

    def begin(self, i):
        for d in (0, 1):
            self.send(d, i)

    def step(self, i):
        for d in (0, 1):
            far, dist = self.order[i]
            sign = 1 if d == 0 else -1
            half = d if far else 1 - d
            self.copy(d, i).wait_recv()
            dest = lax.rem(self.me + self.n + sign * (dist - 1), self.n)
            self.add(dest, half, self.recv.at[d, i])
            if i + 2 <= self.n - 2:
                self.send(d, i + 2)

    def finish(self):
        for i in range(self.n - 1):
            for d in (0, 1):
                self.copy(d, i).wait_send()


def greet(peers):
    barrier = pltpu.get_barrier_semaphore()
    for peer in peers:
        pl.semaphore_signal(barrier, inc=1, device_id=peer, device_id_type=pl.DeviceIdType.MESH)
    pl.semaphore_wait(barrier, len(peers))


def forward_kernel(nz, ny, n_total, x_ref, w1_ref, w2_ref, ht_ref, lab_ref,
                   et_out, ut_hbm, sl_hbm, xt_hbm,
                   p1, p2, ut_v, sl_v, xt_v, ry1, rz1, rz2, ry2, agy, agz, zrow, logit,
                   sy1, vy1, sz1, vz1, sz2, vz2, sy2, vy2, say, vay, saz, vaz, out_sem):
    me = lax.axis_index('model')
    dat = lax.axis_index('data')
    z, y = lax.div(me, ny), lax.rem(me, ny)
    rows = p1.shape[2]
    half_rows = rows // 2
    c1, c2 = p1.shape[3], p2.shape[3]
    blk = ny * rows

    def peer_y(t):
        return (z * ny + t, dat)

    def peer_z(t):
        return (t * ny + y, dat)

    greet([peer_y(lax.rem(y + k, ny)) for k in range(1, ny)] + [peer_z(lax.rem(z + k, nz)) for k in range(1, nz)])

    def hs(half):
        return pl.ds(half * half_rows, half_rows)

    def add_y1(dest, half, buf):
        def body(k, _):
            p1[k, dest, hs(half), :] += buf[k]
            return 0
        lax.fori_loop(0, nz, body, 0)

    def add_z1(dest, half, buf):
        p1[dest, y, hs(half), :] += buf[...]

    def add_z2(dest, half, buf):
        def body(k, _):
            p2[dest, k, hs(half), :] += buf[k]
            return 0
        lax.fori_loop(0, ny, body, 0)

    def add_y2(dest, half, buf):
        p2[z, dest, hs(half), :] += buf[...]

    ring_y1 = Ring(ny, y, peer_y, lambda t, h: p1.at[:, t, hs(h), :], ry1, sy1, vy1, add_y1)
    ring_z1 = Ring(nz, z, peer_z, lambda t, h: p1.at[t, y, hs(h), :], rz1, sz1, vz1, add_z1)
    ring_z2 = Ring(nz, z, peer_z, lambda t, h: p2.at[t, :, hs(h), :], rz2, sz2, vz2, add_z2)
    ring_y2 = Ring(ny, y, peer_y, lambda t, h: p2.at[z, t, hs(h), :], ry2, sy2, vy2, add_y2)

    scale = np.float32(np.sqrt(2.0 / np.pi))

    def block(zz):
        at = pl.ds(pl.multiple_of(zz * blk, blk), blk)
        pre = jnp.dot(x_ref[at, :], w1_ref[...], preferred_element_type=F32)
        square = pre * pre
        th = jnp.tanh(scale * (pre + np.float32(0.044715) * (square * pre)))
        cdf = 0.5 * (1.0 + th)
        act = (pre * cdf).astype(BF16)
        sl_v[at, :] = cdf + 0.5 * pre * (1.0 - th * th) * (scale * (1.0 + np.float32(3 * 0.044715) * square))
        ut_v[:, at] = act.T
        part = jnp.dot(act, w2_ref[...], preferred_element_type=F32)
        p1[zz] = part[:, :c1].reshape(ny, rows, c1)
        p2[zz] = part[:, c1:].reshape(ny, rows, c2)

    far = [nz // 2]
    for k in range(nz // 2 - 1, 0, -1):
        far += [k, nz - k]
    far += [0]

    def run(first, last):
        def body(i, _):
            step = lax.div(i + 1, 2)
            off = nz // 2 + jnp.where(lax.rem(i, 2) == 1, -step, step)
            block(lax.rem(z + off, nz))
            return 0
        lax.fori_loop(first, last, body, 0)

    run(0, 1)
    ring_z2.begin(0)
    run(1, 3)
    ring_z2.begin(1)
    run(3, nz)
    ring_y1.begin(0)
    ring_y1.begin(1)

    out_copies = [pltpu.make_async_copy(ut_v, ut_hbm, out_sem.at[0]), pltpu.make_async_copy(sl_v, sl_hbm, out_sem.at[1])]
    for c in out_copies:
        c.start()

    def flip(i, _):
        at = pl.ds(pl.multiple_of(i * blk, blk), blk)
        xt_v[:, at] = x_ref[at, :].T
        return 0
    lax.fori_loop(0, nz, flip, 0)
    out_copies.append(pltpu.make_async_copy(xt_v, xt_hbm, out_sem.at[2]))
    out_copies[-1].start()

    events = [(10 + 11.3 * (i + 1), 'y1', i) for i in range(ny - 1)]
    events += [(4 + 5.6 * (i + 1), 'z2', i) for i in range(nz - 1)]
    z2_end = 4 + 5.6 * (nz - 1)
    y1_end = 10 + 11.3 * (ny - 1)
    events += [(y1_end + 0.5 + 2.2 * (i + 1), 'z1', i) for i in range(nz - 1)]
    events += [(z2_end + 1 + 3 * (i + 1), 'y2', i) for i in range(ny - 1)]
    rings = {'y1': ring_y1, 'z1': ring_z1, 'z2': ring_z2, 'y2': ring_y2}
    for _, name, i in sorted(events):
        rings[name].step(i)
        if name == 'z2' and i == nz - 2:
            ring_y2.begin(0)
            ring_y2.begin(1)
        if name == 'y1' and i == ny - 2:
            ring_z1.begin(0)
            ring_z1.begin(1)

    mine = pl.ds(pl.multiple_of(me * rows, rows), rows)
    zrow[:, :c1] = (x_ref[mine, :c1].astype(F32) + p1[z, y]).astype(BF16)
    zrow[:, c1:] = (x_ref[mine, c1:].astype(F32) + p2[z, y]).astype(BF16)
    logit[...] = lax.dot_general(ht_ref[...], zrow[...], (((1,), (1,)), ((), ())), preferred_element_type=F32)
    l0, l1, l2 = logit[0:4, :], logit[4:8, :], logit[8:12, :]
    top = jnp.maximum(jnp.maximum(l0, l1), l2)
    e0, e1, e2 = jnp.exp(l0 - top), jnp.exp(l1 - top), jnp.exp(l2 - top)
    total = e0 + e1 + e2
    wide = lab_ref[:, pl.ds(pl.multiple_of(lax.div(me, 128 // rows) * 128, 128), 128)]
    lab = wide[:, :rows]
    for k in range(1, 128 // rows):
        lab = jnp.where(lax.rem(me, 128 // rows) == k, wide[:, k * rows:(k + 1) * rows], lab)
    agy[y] = jnp.zeros((16, 128), F32)
    for c, e in enumerate((e0, e1, e2)):
        agy[y, 4 * c:4 * c + 4, 0:rows] = (e / total - jnp.where(lab == c, 1.0, 0.0)) / n_total

    def gather(n, pos, peer, buf, send_sem, recv_sem):
        sends = []
        for k in range(1, n):
            cp = pltpu.make_async_remote_copy(
                src_ref=buf.at[pos], dst_ref=buf.at[pos], send_sem=send_sem.at[k], recv_sem=recv_sem.at[k],
                device_id=peer(lax.rem(pos + k, n)), device_id_type=pl.DeviceIdType.MESH)
            cp.start()
            sends.append(cp)
        for k in range(1, n):
            src = lax.rem(pos + n - k, n)
            pltpu.make_async_remote_copy(
                src_ref=buf.at[pos], dst_ref=buf.at[src], send_sem=send_sem.at[k], recv_sem=recv_sem.at[k],
                device_id=peer(lax.rem(pos + k, n)), device_id_type=pl.DeviceIdType.MESH).wait_recv()
        return sends

    sends = gather(ny, y, peer_y, agy, say, vay)
    per = 128 // rows
    low = lax.broadcasted_iota(jnp.int32, (16, 128), 1)
    for q in range(ny // per):
        tile = agy[q * per]
        for k in range(1, per):
            tile = jnp.where(low >= k * rows, pltpu.roll(agy[q * per + k], k * rows, 1), tile)
        agz[z, :, q * 128:(q + 1) * 128] = tile
    sends += gather(nz, z, peer_z, agz, saz, vaz)
    for k in range(nz):
        et_out[:, k * blk:(k + 1) * blk] = agz[k]

    for c in sends:
        c.wait_send()
    for ring in rings.values():
        ring.finish()
    for c in out_copies:
        c.wait()


def backward_kernel(nz, ny, nx, x_shape, ut_ref, w2_ref, et_ref, h_ref, sl_hbm, xt_hbm,
                    a_out, g1_out, g2_out,
                    xt_v, sl_v, ecol, dz, da, g1, g2, d1, d2, r1, r2, gram_x, gram_y, gram_z, mat,
                    in_sem, sd, vd, sx, vx, sgx, vgx, sgy, vgy, sgz, vgz):
    me = lax.axis_index('model')
    dat = lax.axis_index('data')
    z, y = lax.div(me, ny), lax.rem(me, ny)
    x, core = lax.div(dat, CORES), lax.rem(dat, CORES)
    nd = nx * CORES
    n_tok, n_dim = x_shape
    n_ffn = ut_ref.shape[0]
    n_task = g1.shape[0]

    loads = [pltpu.make_async_copy(sl_hbm, sl_v, in_sem.at[0]), pltpu.make_async_copy(xt_hbm, xt_v, in_sem.at[1])]
    for c in loads:
        c.start()

    def peer_d(t):
        return (me, t)

    def peer_y(t):
        return (z * ny + t, dat)

    def peer_z(t):
        return (t * ny + y, dat)

    def peer_x(t):
        return (me, t * CORES + core)

    greet([peer_d(lax.rem(dat + k, nd)) for k in range(1, nd)]
          + [peer_y(lax.rem(y + k, ny)) for k in range(1, ny)]
          + [peer_z(lax.rem(z + k, nz)) for k in range(1, nz)])

    other = (me, x * CORES + 1 - core)

    def turn(i, _):
        at = pl.ds(pl.multiple_of(i * 128, 128), 128)
        ecol[at, :] = et_ref[:, at].T
        return 0
    lax.fori_loop(0, n_tok // 128, turn, 0)

    rb = 64

    def make_dz(t):
        def body(i, _):
            at = pl.ds(pl.multiple_of(i * rb, rb), rb)
            acc = ecol[at, t:t + 1] * h_ref[t:t + 1, :]
            for c in (1, 2):
                acc = acc + ecol[at, 4 * c + t:4 * c + t + 1] * h_ref[4 * c + t:4 * c + t + 1, :]
            dz[at, :] = acc.astype(BF16)
            return 0
        lax.fori_loop(0, n_tok // rb, body, 0)

    tile = 256
    q2 = g2.shape[3]
    q1 = g1.shape[3]

    def make_g2(t):
        def body(i, _):
            at = pl.ds(pl.multiple_of(i * tile, tile), tile)
            out = jnp.dot(ut_ref[...], dz[:, at], preferred_element_type=F32)
            g2[t, :, :, :, at] = out.reshape(nx, CORES, q2, tile)
            return 0
        lax.fori_loop(0, n_dim // tile, body, 0)

    def make_da():
        def body(i, _):
            at = pl.ds(pl.multiple_of(i * 2 * tile, 2 * tile), 2 * tile)
            out = lax.dot_general(dz[at, :], w2_ref[...], (((1,), (1,)), ((), ())), preferred_element_type=F32)
            da[at, :] = (out * sl_v[at, :]).astype(BF16)
            return 0
        lax.fori_loop(0, n_tok // (2 * tile), body, 0)

    def make_g1(t):
        def body(i, _):
            at = pl.ds(pl.multiple_of(i * tile, tile), tile)
            for k in (0, 1):
                hx = nx // 2
                rows = pl.ds(k * (n_dim // 2), n_dim // 2)
                out = jnp.dot(xt_v[rows, :], da[:, at], preferred_element_type=F32)
                g1[t, k * hx:(k + 1) * hx, :, :, at] = out.reshape(hx, CORES, q1, tile)
            return 0
        lax.fori_loop(0, n_ffn // tile, body, 0)

    def swap(s, g, buf):
        t = s // 2
        return pltpu.make_async_remote_copy(
            src_ref=g.at[t, :, 1 - core], dst_ref=buf.at[t], send_sem=sd.at[s], recv_sem=vd.at[s],
            device_id=other, device_id_type=pl.DeviceIdType.MESH)

    def add_swap(s, g, buf):
        t = s // 2
        swap(s, g, buf).wait_recv()

        def body(k, _):
            g[t, k, core] += buf[t, k]
            return 0
        lax.fori_loop(0, nx, body, 0)

    def ring_of(s):
        g, r, d = ((g2, r2, d2), (g1, r1, d1))[s % 2]
        t = s // 2
        half_rows = g.shape[3] // 2

        def chunk(dest, half):
            return g.at[t, dest, core, pl.ds(half * half_rows, half_rows), :]

        def add(dest, half, buf):
            g[t, dest, core, pl.ds(half * half_rows, half_rows), :] += buf[...]

        return Ring(nx, x, peer_x, chunk, r.at[t], sx.at[s], vx.at[s], add)

    n_stage = 2 * n_task
    bufs = ((g2, d2), (g1, d1))
    for s in range(n_stage):
        t = s // 2
        if s % 2 == 0:
            make_dz(t)
            make_g2(t)
        else:
            if s == 1:
                loads[0].wait()
            make_da()
            if s == 1:
                loads[1].wait()
            make_g1(t)
        swap(s, *bufs[s % 2]).start()
        if s >= 1:
            add_swap(s - 1, *bufs[(s - 1) % 2])
            ring_of(s - 1).begin(0)
            ring_of(s - 1).begin(1)
    s = n_stage - 1
    add_swap(s, *bufs[s % 2])
    ring_of(s).begin(0)
    ring_of(s).begin(1)
    for s in range(n_stage):
        ring_of(s).step(0)
    for s in range(n_stage):
        ring_of(s).step(1)
        ring_of(s).step(2)

    row_id = lax.broadcasted_iota(jnp.int32, (8, 128), 0)
    col_id = lax.broadcasted_iota(jnp.int32, (8, 128), 1)
    pairs = [(i, j) for i in range(n_task) for j in range(i, n_task)]

    def fold(g, accs):
        width = g.shape[4]

        def body(k, accs):
            at = pl.ds(pl.multiple_of(k * 8, 8), 8)
            vals = [g[t, x, core, at, :] for t in range(n_task)]
            return tuple(acc + sum((vals[i] * vals[j])[:, w:w + 128] for w in range(0, width, 128))
                         for acc, (i, j) in zip(accs, pairs))
        return lax.fori_loop(0, g.shape[3] // 8, body, accs)

    accs = tuple(jnp.zeros((8, 128), F32) for _ in pairs)
    accs = fold(g2, accs)
    accs = fold(g1, accs)
    part = jnp.zeros((8, 128), F32)
    for acc, (i, j) in zip(accs, pairs):
        hit = ((row_id == i) & (col_id == j)) | ((row_id == j) & (col_id == i))
        part = jnp.where(hit, jnp.sum(jnp.sum(acc, axis=1, keepdims=True), axis=0, keepdims=True), part)

    sends = []

    def all_sum(n, pos, peer, buf, send_sem, recv_sem, val):
        buf[pos] = val
        for k in range(1, n):
            cp = pltpu.make_async_remote_copy(
                src_ref=buf.at[pos], dst_ref=buf.at[pos], send_sem=send_sem.at[k], recv_sem=recv_sem.at[k],
                device_id=peer(lax.rem(pos + k, n)), device_id_type=pl.DeviceIdType.MESH)
            cp.start()
            sends.append(cp)
        for k in range(1, n):
            src = lax.rem(pos + n - k, n)
            pltpu.make_async_remote_copy(
                src_ref=buf.at[pos], dst_ref=buf.at[src], send_sem=send_sem.at[k], recv_sem=recv_sem.at[k],
                device_id=peer(lax.rem(pos + k, n)), device_id_type=pl.DeviceIdType.MESH).wait_recv()
        out = buf[0]
        for k in range(1, n):
            out = out + buf[k]
        return out

    part = all_sum(nd, dat, peer_d, gram_x, sgx, vgx, part)
    part = all_sum(ny, y, peer_y, gram_y, sgy, vgy, part)
    gram = all_sum(nz, z, peer_z, gram_z, sgz, vgz, part)

    eye = row_id == col_id
    live = (row_id < n_task) & (col_id < n_task)
    trace = jnp.sum(jnp.sum(jnp.where(eye & live, gram, 0.0), axis=1, keepdims=True), axis=0, keepdims=True)
    scaled = jnp.where(live, gram, 0.0)
    trace_scale = trace / n_task
    wrow = jnp.where(col_id < n_task, 1.0 / n_task, 0.0).astype(F32)
    wcol = jnp.where(row_id < n_task, 1.0 / n_task, 0.0).astype(F32)

    def eg(i, carry):
        wrow, wcol = carry
        prod = jnp.sum(scaled * wrow, axis=1, keepdims=True)
        up = wcol * jnp.exp(-prod / trace_scale)
        new = up / jnp.sum(up, axis=0, keepdims=True)
        return jnp.sum(jnp.where(eye, new, 0.0), axis=0, keepdims=True) + jnp.zeros_like(wrow), new

    wrow, wcol = lax.fori_loop(0, STEPS, eg, (wrow, wcol))
    a_out[...] = wrow
    ws = [jnp.sum(jnp.where((row_id == t) & (col_id == t), wrow, 0.0), keepdims=True)[0:1, 0:1] for t in range(n_task)]

    def mix(g, out):
        def body(k, _):
            at = pl.ds(pl.multiple_of(k * 8, 8), 8)
            acc = ws[0] * g[0, x, core, at, :]
            for t in range(1, n_task):
                acc = acc + ws[t] * g[t, x, core, at, :]
            out[at, :] = acc
            return 0
        lax.fori_loop(0, g.shape[3] // 8, body, 0)
    mix(g1, g1_out)
    mix(g2, g2_out)

    for c in sends:
        c.wait_send()
    for s in range(n_stage):
        swap(s, *bufs[s % 2]).wait_send()
        ring_of(s).finish()


def solution(mesh, ny=NY):
    n_data = mesh.shape['data']
    nz = mesh.shape['model'] // ny
    nx = n_data // CORES

    def local_step(tokens, w_up, w_down, task_heads, labels):
        n_tok, n_dim = tokens.shape
        n_ffn = w_up.shape[1]
        n_task, _, n_class = task_heads.shape
        rows = n_tok // (nz * ny)
        hr = rows // 2
        c1 = n_dim // 2
        c2 = n_dim - c1
        heads = jnp.transpose(task_heads, (2, 0, 1)).reshape(n_class * n_task, n_dim)
        heads = jnp.pad(heads, ((0, 16 - n_class * n_task), (0, 0)))
        vm = pl.BlockSpec(memory_space=pltpu.VMEM)
        hbm = pl.BlockSpec(memory_space=pl.ANY)
        dma = pltpu.SemaphoreType.DMA

        et, ut, slope, xt = pl.pallas_call(
            functools.partial(forward_kernel, nz, ny, n_tok * n_data),
            out_shape=[jax.ShapeDtypeStruct((16, n_tok), F32), jax.ShapeDtypeStruct((n_ffn, n_tok), BF16),
                       jax.ShapeDtypeStruct((n_tok, n_ffn), F32), jax.ShapeDtypeStruct((n_dim, n_tok), BF16)],
            in_specs=[vm] * 5, out_specs=[vm, hbm, hbm, hbm],
            scratch_shapes=[
                pltpu.VMEM((nz, ny, rows, c1), F32), pltpu.VMEM((nz, ny, rows, c2), F32),
                pltpu.VMEM((n_ffn, n_tok), BF16), pltpu.VMEM((n_tok, n_ffn), F32), pltpu.VMEM((n_dim, n_tok), BF16),
                pltpu.VMEM((2, ny - 1, nz, hr, c1), F32), pltpu.VMEM((2, nz - 1, hr, c1), F32),
                pltpu.VMEM((2, nz - 1, ny, hr, c2), F32), pltpu.VMEM((2, ny - 1, hr, c2), F32),
                pltpu.VMEM((ny, 16, 128), F32), pltpu.VMEM((nz, 16, ny * rows), F32),
                pltpu.VMEM((rows, n_dim), BF16), pltpu.VMEM((16, rows), F32),
                dma((2, ny - 1)), dma((2, ny - 1)), dma((2, nz - 1)), dma((2, nz - 1)),
                dma((2, nz - 1)), dma((2, nz - 1)), dma((2, ny - 1)), dma((2, ny - 1)),
                dma((ny,)), dma((ny,)), dma((nz,)), dma((nz,)), dma((3,))],
            compiler_params=pltpu.CompilerParams(collective_id=0, has_side_effects=True, vmem_limit_bytes=VMEM_LIMIT),
            name='forward',
        )(tokens, w_up, w_down, heads, labels)

        r1 = n_dim // n_data
        r2 = n_ffn // n_data
        a_tile, g1, g2 = pl.pallas_call(
            functools.partial(backward_kernel, nz, ny, nx, (n_tok, n_dim)),
            out_shape=[jax.ShapeDtypeStruct((8, 128), F32), jax.ShapeDtypeStruct((r1, n_ffn), F32),
                       jax.ShapeDtypeStruct((r2, n_dim), F32)],
            in_specs=[vm] * 4 + [hbm, hbm], out_specs=[vm, vm, vm],
            scratch_shapes=[
                pltpu.VMEM((n_dim, n_tok), BF16), pltpu.VMEM((n_tok, n_ffn), F32), pltpu.VMEM((n_tok, 16), F32),
                pltpu.VMEM((n_tok, n_dim), BF16), pltpu.VMEM((n_tok, n_ffn), BF16),
                pltpu.VMEM((n_task, nx, CORES, r1, n_ffn), F32), pltpu.VMEM((n_task, nx, CORES, r2, n_dim), F32),
                pltpu.VMEM((n_task, nx, r1, n_ffn), F32), pltpu.VMEM((n_task, nx, r2, n_dim), F32),
                pltpu.VMEM((n_task, 2, nx - 1, r1 // 2, n_ffn), F32), pltpu.VMEM((n_task, 2, nx - 1, r2 // 2, n_dim), F32),
                pltpu.VMEM((n_data, 8, 128), F32), pltpu.VMEM((ny, 8, 128), F32), pltpu.VMEM((nz, 8, 128), F32),
                pltpu.VMEM((8, 128), F32),
                dma((2,)), dma((2 * n_task,)), dma((2 * n_task,)),
                dma((2 * n_task, 2, nx - 1)), dma((2 * n_task, 2, nx - 1)),
                dma((n_data,)), dma((n_data,)), dma((ny,)), dma((ny,)), dma((nz,)), dma((nz,))],
            compiler_params=pltpu.CompilerParams(collective_id=1, has_side_effects=True, vmem_limit_bytes=VMEM_LIMIT),
            name='backward',
        )(ut, w_down, et, heads.astype(F32), slope, xt)
        return a_tile[0, :n_task], g1, g2

    return jax.shard_map(
        local_step, mesh=mesh,
        in_specs=(P('data', None), P(None, 'model'), P('model', None), P(None, None, None), P(None, 'data')),
        out_specs=(P(None), P('data', 'model'), P(('model', 'data'), None)),
        check_vma=False)
```

time: 588 us -> 199 us (0.34); the launches traced: 582 us -> 199 us
  waiting for transfers between devices: 340 us -> 0 us
  Pallas kernels: 0 us -> 192 us
  matrix products: 91.8 us -> 0 us
  blocking collectives: 76.7 us -> 0 us
  other arithmetic: 28.4 us -> 0.65 us
  local copies, waits for them, and re-layouts: 27.9 us -> 5.28 us
  between operations: 15.5 us -> 0.65 us
    psum x1 -> x0, waiting for transfers between devices: 215 us -> none  [local_step(): mlp_out = lax.psum(part_out, 'model')]
    pallas_call x0 -> x2, Pallas kernels: none -> 192 us  [the longest x1 116 us: local_step(): pl.pallas_call(functools.partial(backward_kernel, nz, ny, nx, (n_tok, n_d...]
    dot_general x10 -> x0, matrix products: 91.8 us -> none  [the longest x1 25.6 us: local_step(): jnp.einsum('bd,tbf->tdf', tokens, d_pre, preferred_element_type=jnp.float32)]
    psum x1 -> x0, blocking collectives: 76.7 us -> none  [local_step(): gram_mat = lax.psum(gram_part, ('model', 'data'))]
    unnamed x4 -> x0, waiting for transfers between devices: 74.8 us -> none
    reduce_scatter x1 -> x0, waiting for transfers between devices: 50.8 us -> none  [local_step(): up_shard = lax.psum_scatter(g_up, 'data', scatter_dimension=1, tiled=True)]
    reduce_sum x42 -> x0, other arithmetic: 15.3 us -> none  [the longest x20 12.4 us: eg_step(): return updated / jnp.sum(updated)]
    div x21 -> x0, other arithmetic: 13 us -> none  [the longest x20 13 us: eg_step(): return updated / jnp.sum(updated)]
  transfers between devices with their start and end apart: 3 -> 0, of which waited for: 3 -> 0; matrix products, arithmetic and copies ran while one was open for 7% -> 0% of each run, Pallas kernels for 0% -> 0%
where the time goes in v1:
time: 199 us
  Pallas kernels  192 us (96%)
  local copies, waits for them, and re-layouts  5.28 us (3%)
    pallas_call x1, Pallas kernels, local_step(): pl.pallas_call(functools.partial(backward_kernel, nz, ny, nx, (n_tok, n_d...  116 us
    pallas_call x1, Pallas kernels, local_step(): pl.pallas_call(functools.partial(forward_kernel, nz, ny, n_tok * n_data),...  76.8 us

profile of v1, /device:TPU:1, one launch (start us, length us, event | category | flops | bytes accessed | tf_op | source)
XLA Modules:
  0.0 198.9 jit_solution(4260121080368304446)
XLA Ops:
  0.6 0.8 reshape.9
  1.4 0.6 pad_convert_fusion
  2.0 76.8 %forward.1 = (f32[16,2048]{1,0:T(8,128)}, bf16[512,2048]{1,0:T(8,128)(2,1)}, f32[2048,512]{1,0:T(8,128)}, bf16[1024,2048]{1,0:T(8,128)(2,1)}) custom-call(bf16[2048,1024]{1,0:T(8,128)(2,1)} %x_ref.1, bf16[1024,512]{1,0:T(8,128)(2,1)} %w1_ref.1, bf16[512,1024]{1,0:T(8,128)(2,1)} %w2_ref.3, bf16[16,1024]{1,0:T(8,128)(2,1)} %get-tuple-element.18.ht_ref, ...), custom_call_target="tpu_custom_call" | custom-call | tf_op jit(solution)/shard_map/forward/pallas_call | solution.py:476
  78.8 115.6 %backward.1 = (f32[8,128]{1,0:T(8,128)}, f32[128,512]{1,0:T(8,128)}, f32[64,1024]{1,0:T(8,128)}) custom-call(bf16[512,2048]{1,0:T(8,128)(2,1)} %get-tuple-element.10.ut_ref, bf16[512,1024]{1,0:T(8,128)(2,1)} %w2_ref.3, f32[16,2048]{1,0:T(8,128)} %get-tuple-element.11.et_ref, f32[16,1024]{1,0:T(8,128)} %get-tuple-element.17.h_ref, ...), custom_call_target="tpu_custom_call" | custom-call | tf_op jit(solution)/shard_map/backward/pallas_call | solution.py:497
  194.4 1.2 slice_bitcast_fusion
  195.6 1.7 copy.10
  197.3 1.7 copy.11

commit v2 on v0

v2 whole, which is shorter than its diff:
```python
import functools

import jax
import jax.numpy as jnp
import numpy as np
from jax import lax
from jax.experimental import pallas as pl
from jax.experimental.pallas import tpu as pltpu
from jax.sharding import PartitionSpec as P

STEPS = 20
NY = 4
CORES = 2
F32 = jnp.float32
BF16 = jnp.bfloat16
VMEM_LIMIT = 67043328


def chain(n):
    return [(i % 2 == 0, n // 2 - (i + 1) // 2) for i in range(n - 1)]


class Ring:
    def __init__(self, n, me, peer, chunk, recv, send_sem, recv_sem, add):
        self.n, self.me, self.peer, self.chunk = n, me, peer, chunk
        self.recv, self.send_sem, self.recv_sem, self.add = recv, send_sem, recv_sem, add
        self.order = chain(n)

    def copy(self, d, i):
        far, dist = self.order[i]
        sign = 1 if d == 0 else -1
        half = d if far else 1 - d
        dest = lax.rem(self.me + self.n + sign * dist, self.n)
        target = lax.rem(self.me + self.n + sign, self.n)
        return pltpu.make_async_remote_copy(
            src_ref=self.chunk(dest, half, sign * dist % self.n), dst_ref=self.recv.at[d, i],
            send_sem=self.send_sem.at[d, i], recv_sem=self.recv_sem.at[d, i],
            device_id=self.peer(target), device_id_type=pl.DeviceIdType.MESH)

    def send(self, d, i):
        self.copy(d, i).start()

    def begin(self, i):
        for d in (0, 1):
            self.send(d, i)

    def step(self, i):
        for d in (0, 1):
            far, dist = self.order[i]
            sign = 1 if d == 0 else -1
            half = d if far else 1 - d
            self.copy(d, i).wait_recv()
            dest = lax.rem(self.me + self.n + sign * (dist - 1), self.n)
            self.add(dest, half, sign * (dist - 1) % self.n, self.recv.at[d, i])
            if i + 2 <= self.n - 2:
                self.send(d, i + 2)

    def finish(self):
        for i in range(self.n - 1):
            for d in (0, 1):
                self.copy(d, i).wait_send()


def trunk_kernel(nz, ny, nx, n_total, x_hbm, w1_hbm, w2_hbm, ht_ref, lab_ref,
                 a_out, g1_out, g2_out,
                 xd, w1_v, w2_v, ht_v, hb, gg2, gg1, ut_v, sl_v, xt_v, da, ecol,
                 rya, ryb, ryc, rz1, rz2, ry2, agy, agz, zrow, logit,
                 d1, d2, r1, r2, gram_d, gram_m, m1, m2,
                 sya, vya, syb, vyb, syc, vyc, sz1, vz1, sz2, vz2, sy2, vy2, say, vay, saz, vaz,
                 w_sem, x_sem, sd, vd, sx, vx, sgd, vgd, sgm, vgm, o_sem):
    me = lax.axis_index('model')
    dat = lax.axis_index('data')
    z, y = lax.div(me, ny), lax.rem(me, ny)
    x, core = lax.div(dat, CORES), lax.rem(dat, CORES)
    n_model, nd = nz * ny, nx * CORES
    rows, n_dim = gg2.shape[2], gg2.shape[3]
    n_tok, n_ffn = sl_v.shape
    n_task = gg2.shape[0] // CORES
    half_rows = rows // 2
    c1 = rya.shape[4]
    blk = ny * rows

    def peer_y(t):
        return (z * ny + t, dat)

    def peer_z(t):
        return (t * ny + y, dat)

    def peer_m(t):
        return (t, dat)

    def peer_d(t):
        return (me, t)

    def peer_x(t):
        return (me, t * CORES + core)

    other = (me, x * CORES + 1 - core)

    def offset(i):
        step = lax.div(i + 1, 2)
        return nz // 2 + jnp.where(lax.rem(i, 2) == 1, -step, step)

    def block_rows(i):
        return pl.ds(pl.multiple_of(lax.rem(z + offset(i), nz) * blk, blk), blk)

    def load_x(i):
        at = block_rows(i)
        return pltpu.make_async_copy(x_hbm.at[at, :], xd.at[at, :], x_sem.at[i])

    load_w1 = pltpu.make_async_copy(w1_hbm, w1_v, w_sem.at[0])
    load_w2 = pltpu.make_async_copy(w2_hbm, w2_v, w_sem.at[1])
    load_w1.start()
    load_x(0).start()
    load_w2.start()

    def start_x(i, _):
        load_x(i).start()
        return 0
    lax.fori_loop(1, nz, start_x, 0)

    barrier = pltpu.get_barrier_semaphore()
    greeted = [peer_d(lax.rem(dat + k, nd)) for k in range(1, nd)]
    greeted += [peer_m(lax.rem(me + k, n_model)) for k in range(1, n_model)]
    for peer in greeted:
        pl.semaphore_signal(barrier, inc=1, device_id=peer, device_id_type=pl.DeviceIdType.MESH)

    def hs(half):
        return pl.ds(half * half_rows, half_rows)

    left, right = pl.ds(0, c1), pl.ds(c1, n_dim - c1)

    def slot(off):
        return 2 * (nz // 2 - off) - 1 if off < nz // 2 else 2 * (off - nz // 2)

    own = slot(0)

    def add_y1(first):
        def add(dest, half, off, buf):
            def body(k, _):
                gg2[first + k, dest, hs(half), left] += buf[k]
                return 0
            lax.fori_loop(0, buf.shape[0], body, 0)
        return add

    def add_z1(dest, half, off, buf):
        gg2[slot(off), y, hs(half), left] += buf[...]

    def add_z2(dest, half, off, buf):
        def body(k, _):
            gg2[slot(off), k, hs(half), right] += buf[k]
            return 0
        lax.fori_loop(0, ny, body, 0)

    def add_y2(dest, half, off, buf):
        gg2[own, dest, hs(half), right] += buf[...]

    rings = {
        'z1': Ring(nz, z, peer_z, lambda t, h, o: gg2.at[slot(o), y, hs(h), left], rz1, sz1, vz1, add_z1),
        'z2': Ring(nz, z, peer_z, lambda t, h, o: gg2.at[slot(o), :, hs(h), right], rz2, sz2, vz2, add_z2),
        'y2': Ring(ny, y, peer_y, lambda t, h, o: gg2.at[own, t, hs(h), right], ry2, sy2, vy2, add_y2),
    }
    first = 0
    for name, recv, send_sem, recv_sem in (('ya', rya, sya, vya), ('yb', ryb, syb, vyb), ('yc', ryc, syc, vyc)):
        group = pl.ds(first, recv.shape[2])
        rings[name] = Ring(ny, y, peer_y, lambda t, h, o, group=group: gg2.at[group, t, hs(h), left],
                           recv, send_sem, recv_sem, add_y1(first))
        first += recv.shape[2]

    scale = np.float32(np.sqrt(2.0 / np.pi))

    def block(i, _):
        load_x(i).wait()
        at = block_rows(i)
        pre = jnp.dot(xd[at, :], w1_v[...], preferred_element_type=F32)
        square = pre * pre
        th = jnp.tanh(scale * (pre + np.float32(0.044715) * (square * pre)))
        cdf = 0.5 * (1.0 + th)
        act = (pre * cdf).astype(BF16)
        sl_v[at, :] = cdf + 0.5 * pre * (1.0 - th * th) * (scale * (1.0 + np.float32(3 * 0.044715) * square))
        ut_v[:, at] = act.T
        part = jnp.dot(act, w2_v[...], preferred_element_type=F32)
        gg2[i] = part.reshape(ny, rows, n_dim)
        return 0

    load_w1.wait()
    load_w2.wait()
    block(0, 0)
    pl.semaphore_wait(barrier, len(greeted))
    rings['z2'].begin(0)
    lax.fori_loop(1, 3, block, 0)
    rings['ya'].begin(0)
    rings['z2'].begin(1)
    rings['ya'].begin(1)
    lax.fori_loop(3, nz, block, 0)

    def flip(i, _):
        at = pl.ds(pl.multiple_of(i * blk, blk), blk)
        xt_v[:, at] = xd[at, :].T
        return 0
    lax.fori_loop(0, nz, flip, 0)
    n_head = ht_ref.shape[0]
    ht_v[...] = jnp.zeros_like(ht_v)
    ht_v[0:n_head, :] = ht_ref[...]
    for k in range(n_head):
        hb[k] = jnp.broadcast_to(ht_v[k:k + 1, :].astype(F32), (8, n_dim))

    order = [
        ('z2', 0), ('ya', 0), ('z2', 1), ('z2', 2), ('ya', 1), ('z2', 3), ('ya', 2), ('z2', 4), ('yb', 0), ('z1', 0),
        ('yb', 1), ('z2', 5), ('yb', 2), ('z1', 1), ('z1', 2), ('z2', 6), ('yc', 0), ('yc', 1), ('y2', 0), ('y2', 1),
        ('yc', 2), ('z1', 3), ('z1', 4), ('y2', 2), ('z1', 5), ('z1', 6)]
    begins = {('ya', 0): 'yb', ('ya', 2): 'z1', ('yb', 0): 'yc', ('z2', 6): 'y2'}
    for event in order:
        name, i = event
        rings[name].step(i)
        if event in begins:
            rings[begins[event]].begin(0)
            rings[begins[event]].begin(1)

    mine = pl.ds(pl.multiple_of(me * rows, rows), rows)
    zrow[...] = (xd[mine, :].astype(F32) + gg2[own, y]).astype(BF16)
    logit[...] = lax.dot_general(ht_v[...], zrow[...], (((1,), (1,)), ((), ())), preferred_element_type=F32)
    l0, l1, l2 = logit[0:4, :], logit[4:8, :], logit[8:12, :]
    top = jnp.maximum(jnp.maximum(l0, l1), l2)
    e0, e1, e2 = jnp.exp(l0 - top), jnp.exp(l1 - top), jnp.exp(l2 - top)
    total = e0 + e1 + e2
    per = 128 // rows
    wide = lab_ref[:, pl.ds(pl.multiple_of(lax.div(me, per) * 128, 128), 128)]
    lab = wide[:, :rows]
    for k in range(1, per):
        lab = jnp.where(lax.rem(me, per) == k, wide[:, k * rows:(k + 1) * rows], lab)
    agy[y] = jnp.zeros((16, 128), F32)
    for c, e in enumerate((e0, e1, e2)):
        agy[y, 4 * c:4 * c + 4, 0:rows] = (e / total - jnp.where(lab == c, 1.0, 0.0)) / n_total

    sends = []

    def exchange(n, pos, peer, view, send_sem, recv_sem, use=None):
        def copy(k, src):
            return pltpu.make_async_remote_copy(
                src_ref=view(pos), dst_ref=view(src), send_sem=send_sem.at[k], recv_sem=recv_sem.at[k],
                device_id=peer(lax.rem(pos + k, n)), device_id_type=pl.DeviceIdType.MESH)
        for k in range(1, n):
            cp = copy(k, pos)
            cp.start()
            sends.append(cp)
        if use:
            use(pos)
        for k in range(1, n):
            src = lax.rem(pos + n - k, n)
            copy(k, src).wait_recv()
            if use:
                use(src)

    exchange(ny, y, peer_y, lambda p: agy.at[p], say, vay)
    low = lax.broadcasted_iota(jnp.int32, (16, 128), 1)
    for q in range(ny // per):
        tile = agy[q * per]
        for k in range(1, per):
            tile = jnp.where(low >= k * rows, pltpu.roll(agy[q * per + k], k * rows, 1), tile)
        agz[z, :, q * 128:(q + 1) * 128] = tile

    def turn(k):
        ecol[pl.ds(pl.multiple_of(k * blk, blk), blk), :] = agz[k].T

    exchange(nz, z, peer_z, lambda p: agz.at[p], saz, vaz, turn)
    for ring in rings.values():
        ring.finish()

    rb = 64

    def make_dz(t):
        def body(i, _):
            at = pl.ds(pl.multiple_of(i * rb, rb), rb)
            es = [jnp.broadcast_to(ecol[at, 4 * c + t:4 * c + t + 1], (rb, 128)) for c in range(3)]
            for j in range(0, n_dim, 128):
                hs3 = [jnp.concatenate([hb[4 * c + t, :, j:j + 128]] * (rb // 8), axis=0) for c in range(3)]
                xd[at, j:j + 128] = (es[0] * hs3[0] + es[1] * hs3[1] + es[2] * hs3[2]).astype(BF16)
            return 0
        lax.fori_loop(0, n_tok // rb, body, 0, unroll=4)

    tile = 256
    q1 = gg1.shape[2]

    def make_g2(t):
        def body(i, _):
            at = pl.ds(pl.multiple_of(i * tile, tile), tile)
            out = jnp.dot(ut_v[...], xd[:, at], preferred_element_type=F32).reshape(nx, CORES, rows, tile)
            for c in range(CORES):
                gg2[CORES * t + c, :, :, at] = out[:, c]
            return 0
        lax.fori_loop(0, n_dim // tile, body, 0)

    def make_da():
        def body(i, _):
            at = pl.ds(pl.multiple_of(i * 2 * tile, 2 * tile), 2 * tile)
            out = lax.dot_general(xd[at, :], w2_v[...], (((1,), (1,)), ((), ())), preferred_element_type=F32)
            da[at, :] = (out * sl_v[at, :]).astype(BF16)
            return 0
        lax.fori_loop(0, n_tok // (2 * tile), body, 0)

    def make_g1(t):
        hx = nx // 2

        def body(i, _):
            at = pl.ds(pl.multiple_of(i * tile, tile), tile)
            for k in (0, 1):
                part = pl.ds(k * (n_dim // 2), n_dim // 2)
                out = jnp.dot(xt_v[part, :], da[:, at], preferred_element_type=F32).reshape(hx, CORES, q1, tile)
                for c in range(CORES):
                    gg1[CORES * t + c, k * hx:(k + 1) * hx, :, at] = out[:, c]
            return 0
        lax.fori_loop(0, n_ffn // tile, body, 0)

    n_stage = 2 * n_task
    sets = ((gg2, d2, r2), (gg1, d1, r1))

    def swap(s):
        g, buf, _ = sets[s % 2]
        t = s // 2
        return pltpu.make_async_remote_copy(
            src_ref=g.at[CORES * t + 1 - core], dst_ref=buf.at[t], send_sem=sd.at[s], recv_sem=vd.at[s],
            device_id=other, device_id_type=pl.DeviceIdType.MESH)

    def ring_of(s):
        g, _, r = sets[s % 2]
        t = s // 2
        half = g.shape[2] // 2

        def chunk(dest, h, off):
            return g.at[CORES * t + core, dest, pl.ds(h * half, half), :]

        def add(dest, h, off, buf):
            g[CORES * t + core, dest, pl.ds(h * half, half), :] += buf[...]

        return Ring(nx, x, peer_x, chunk, r.at[t], sx.at[s], vx.at[s], add)

    def launch(s):
        g, buf, _ = sets[s % 2]
        t = s // 2
        swap(s).wait_recv()

        def body(k, _):
            g[CORES * t + core, k] += buf[t, k]
            return 0
        lax.fori_loop(0, nx, body, 0)
        if s >= 2:
            ring_of(s - 2).step(0)
        ring_of(s).begin(0)
        ring_of(s).begin(1)

    for s in range(n_stage):
        t = s // 2
        if s % 2 == 0:
            make_dz(t)
            if s >= 1:
                launch(s - 1)
            make_g2(t)
        else:
            make_da()
            launch(s - 1)
            make_g1(t)
        swap(s).start()
    launch(n_stage - 1)
    for s in (n_stage - 2, n_stage - 1):
        ring_of(s).step(0)
    for s in range(n_stage):
        ring_of(s).step(1)
        ring_of(s).step(2)

    pairs = [(i, j) for i in range(n_task) for j in range(i, n_task)]

    def fold(g, accs):
        width = g.shape[3]

        def body(k, accs):
            at = pl.ds(pl.multiple_of(k * 8, 8), 8)
            vals = [g[CORES * t + core, x, at, :] for t in range(n_task)]
            return tuple(acc + sum((vals[i] * vals[j])[:, w:w + 128] for w in range(0, width, 128))
                         for acc, (i, j) in zip(accs, pairs))
        return lax.fori_loop(0, g.shape[2] // 8, body, accs)

    accs = tuple(jnp.zeros((8, 128), F32) for _ in pairs)
    accs = fold(gg2, accs)
    accs = fold(gg1, accs)
    lane = lax.broadcasted_iota(jnp.int32, (1, 128), 1)
    part = jnp.zeros((1, 128), F32)
    for acc, (i, j) in zip(accs, pairs):
        hit = (lane == n_task * i + j) | (lane == n_task * j + i)
        part = jnp.where(hit, jnp.sum(jnp.sum(acc, axis=0, keepdims=True), axis=1, keepdims=True), part)

    def all_sum(n, pos, peer, buf, send_sem, recv_sem, val):
        buf[pos, 0:1, :] = val
        exchange(n, pos, peer, lambda p: buf.at[p, pl.ds(0, 1), :], send_sem, recv_sem)
        out = buf[0, 0:1, :]
        for k in range(1, n):
            out = out + buf[k, 0:1, :]
        return out

    part = all_sum(nd, dat, peer_d, gram_d, sgd, vgd, part)
    part = all_sum(n_model, me, peer_m, gram_m, sgm, vgm, part)

    row_id = lax.broadcasted_iota(jnp.int32, (8, 128), 0)
    col_id = lax.broadcasted_iota(jnp.int32, (8, 128), 1)
    eye = row_id == col_id
    wide8 = jnp.broadcast_to(part, (8, 128))
    gram = jnp.zeros((8, 128), F32)
    for t in range(n_task):
        moved = pltpu.roll(wide8, 128 - n_task * t, 1) if t else wide8
        gram = jnp.where((row_id == t) & (col_id < n_task), moved, gram)
    trace = jnp.sum(jnp.sum(jnp.where(eye, gram, 0.0), axis=1, keepdims=True), axis=0, keepdims=True)
    trace_scale = trace / n_task
    wrow = jnp.where(col_id < n_task, 1.0 / n_task, 0.0).astype(F32)
    wcol = jnp.where(row_id < n_task, 1.0 / n_task, 0.0).astype(F32)

    def eg(i, carry):
        wrow, wcol = carry
        prod = jnp.sum(gram * wrow, axis=1, keepdims=True)
        up = wcol * jnp.exp(-prod / trace_scale)
        new = up / jnp.sum(up, axis=0, keepdims=True)
        return jnp.sum(jnp.where(eye, new, 0.0), axis=0, keepdims=True) + jnp.zeros_like(wrow), new

    wrow, wcol = lax.fori_loop(0, STEPS, eg, (wrow, wcol))
    a_out[...] = wrow
    writes = []
    ws = [wcol[t:t + 1, :] for t in range(n_task)]

    def mix(g, out):
        width = g.shape[3]

        def body(k, _):
            at = pl.ds(pl.multiple_of(k * 8, 8), 8)
            for w in range(0, width, 128):
                acc = ws[0] * g[core, x, at, w:w + 128]
                for t in range(1, n_task):
                    acc = acc + ws[t] * g[CORES * t + core, x, at, w:w + 128]
                out[at, w:w + 128] = acc
            return 0
        lax.fori_loop(0, g.shape[2] // 8, body, 0)
    for k, (g, stage_out, out) in enumerate(((gg1, m1, g1_out), (gg2, m2, g2_out))):
        mix(g, stage_out)
        writes.append(pltpu.make_async_copy(stage_out, out, o_sem.at[k]))
        writes[-1].start()

    for c in writes:
        c.wait()
    for c in sends:
        c.wait_send()
    for s in range(n_stage):
        swap(s).wait_send()
        ring_of(s).finish()


def write_kernel(a_ref, g1_ref, g2_ref, a_out, g1_out, g2_out):
    a_out[...] = a_ref[0:1, 0:a_out.shape[1]]
    g1_out[...] = g1_ref[...]
    g2_out[...] = g2_ref[...]


def solution(mesh, ny=NY):
    n_data = mesh.shape['data']
    n_model = mesh.shape['model']
    nz = n_model // ny
    nx = n_data // CORES

    def local_step(tokens, w_up, w_down, task_heads, labels):
        n_tok, n_dim = tokens.shape
        n_ffn = w_up.shape[1]
        n_task, _, n_class = task_heads.shape
        rows = n_tok // n_model
        hr = rows // 2
        c1 = 5 * n_dim // 8
        c2 = n_dim - c1
        f1 = n_dim // n_data
        f2 = n_ffn // n_data
        heads = jnp.transpose(task_heads, (2, 0, 1)).reshape(n_class * n_task, n_dim)
        vm = pl.BlockSpec(memory_space=pltpu.VMEM)
        hbm = pl.BlockSpec(memory_space=pl.ANY)
        dma = pltpu.SemaphoreType.DMA
        outs = [jax.ShapeDtypeStruct((f1, n_ffn), F32), jax.ShapeDtypeStruct((f2, n_dim), F32)]
        stages = 2 * n_task

        results = pl.pallas_call(
            functools.partial(trunk_kernel, nz, ny, nx, n_tok * n_data),
            out_shape=[jax.ShapeDtypeStruct((8, 128), F32)] + outs,
            in_specs=[hbm] * 3 + [vm] * 2, out_specs=[vm, hbm, hbm],
            scratch_shapes=[
                pltpu.VMEM((n_tok, n_dim), BF16), pltpu.VMEM((n_dim, n_ffn), BF16), pltpu.VMEM((n_ffn, n_dim), BF16),
                pltpu.VMEM((16, n_dim), BF16), pltpu.VMEM((n_class * n_task, 8, n_dim), F32),
                pltpu.VMEM((CORES * n_task, nx, f2, n_dim), F32), pltpu.VMEM((CORES * n_task, nx, f1, n_ffn), F32),
                pltpu.VMEM((n_ffn, n_tok), BF16), pltpu.VMEM((n_tok, n_ffn), F32), pltpu.VMEM((n_dim, n_tok), BF16),
                pltpu.VMEM((n_tok, n_ffn), BF16), pltpu.VMEM((n_tok, 16), F32),
                pltpu.VMEM((2, ny - 1, 3, hr, c1), F32), pltpu.VMEM((2, ny - 1, nz - 6, hr, c1), F32),
                pltpu.VMEM((2, ny - 1, 3, hr, c1), F32), pltpu.VMEM((2, nz - 1, hr, c1), F32),
                pltpu.VMEM((2, nz - 1, ny, hr, c2), F32), pltpu.VMEM((2, ny - 1, hr, c2), F32),
                pltpu.VMEM((ny, 16, 128), F32), pltpu.VMEM((nz, 16, ny * rows), F32),
                pltpu.VMEM((rows, n_dim), BF16), pltpu.VMEM((16, rows), F32),
                pltpu.VMEM((n_task, nx, f1, n_ffn), F32), pltpu.VMEM((n_task, nx, f2, n_dim), F32),
                pltpu.VMEM((n_task, 2, nx - 1, f1 // 2, n_ffn), F32), pltpu.VMEM((n_task, 2, nx - 1, f2 // 2, n_dim), F32),
                pltpu.VMEM((n_data, 8, 128), F32), pltpu.VMEM((n_model, 8, 128), F32),
                pltpu.VMEM((f1, n_ffn), F32), pltpu.VMEM((f2, n_dim), F32),
                *[dma((2, ny - 1))] * 6, dma((2, nz - 1)), dma((2, nz - 1)),
                dma((2, nz - 1)), dma((2, nz - 1)), dma((2, ny - 1)), dma((2, ny - 1)),
                dma((ny,)), dma((ny,)), dma((nz,)), dma((nz,)),
                dma((2,)), dma((nz,)), dma((stages,)), dma((stages,)), dma((stages, 2, nx - 1)), dma((stages, 2, nx - 1)),
                dma((n_data,)), dma((n_data,)), dma((n_model,)), dma((n_model,)), dma((2,))],
            compiler_params=pltpu.CompilerParams(collective_id=0, has_side_effects=True, vmem_limit_bytes=VMEM_LIMIT),
            name='trunk',
        )(tokens, w_up, w_down, heads, labels)
        weights, g1, g2 = pl.pallas_call(
            write_kernel, out_shape=[jax.ShapeDtypeStruct((1, n_task), F32)] + outs,
            in_specs=[vm] * 3, out_specs=[vm] * 3, name='write',
        )(*results)
        return weights.reshape(n_task), g1, g2

    return jax.shard_map(
        local_step, mesh=mesh,
        in_specs=(P('data', None), P(None, 'model'), P('model', None), P(None, None, None), P(None, 'data')),
        out_specs=(P(None), P('data', 'model'), P(('model', 'data'), None)),
        check_vma=False)
```

time: 588 us -> 174 us (0.30)
  waiting for transfers between devices: 340 us -> 0 us
  Pallas kernels: 0 us -> 172 us
  matrix products: 91.8 us -> 0 us
  blocking collectives: 76.7 us -> 0 us
  other arithmetic: 28.4 us -> 0 us
  local copies, waits for them, and re-layouts: 27.9 us -> 1.36 us
  between operations: 15.5 us -> 0.64 us
    psum x1 -> x0, waiting for transfers between devices: 215 us -> none  [local_step(): mlp_out = lax.psum(part_out, 'model')]
    pallas_call x0 -> x2, Pallas kernels: none -> 172 us  [the longest x1 170 us: local_step(): pl.pallas_call(functools.partial(trunk_kernel, nz, ny, nx, n_tok * n_data...]
    dot_general x10 -> x0, matrix products: 91.8 us -> none  [the longest x1 25.6 us: local_step(): jnp.einsum('bd,tbf->tdf', tokens, d_pre, preferred_element_type=jnp.float32)]
    psum x1 -> x0, blocking collectives: 76.7 us -> none  [local_step(): gram_mat = lax.psum(gram_part, ('model', 'data'))]
    unnamed x4 -> x0, waiting for transfers between devices: 74.8 us -> none
    reduce_scatter x1 -> x0, waiting for transfers between devices: 50.8 us -> none  [local_step(): up_shard = lax.psum_scatter(g_up, 'data', scatter_dimension=1, tiled=True)]
    reduce_sum x42 -> x0, other arithmetic: 15.3 us -> none  [the longest x20 12.4 us: eg_step(): return updated / jnp.sum(updated)]
    div x21 -> x0, other arithmetic: 13 us -> none  [the longest x20 13 us: eg_step(): return updated / jnp.sum(updated)]
  transfers between devices with their start and end apart: 3 -> 0, of which waited for: 3 -> 0; matrix products, arithmetic and copies ran while one was open for 7% -> 0% of each run, Pallas kernels for 0% -> 0%
where the time goes in v2:
time: 174 us
  Pallas kernels  172 us (99%)
    pallas_call x1, Pallas kernels, local_step(): pl.pallas_call(functools.partial(trunk_kernel, nz, ny, nx, n_tok * n_data...  170 us

profile of v2, /device:TPU:1, one launch (start us, length us, event | category | flops | bytes accessed | tf_op | source)
XLA Modules:
  0.0 173.6 jit_solution(18216362351495585831)
XLA Ops:
  0.6 1.4 reshape.12.ht_ref
  2.0 169.8 %trunk.1 = (f32[8,128]{1,0:T(8,128)}, f32[128,512]{1,0:T(8,128)}, f32[64,1024]{1,0:T(8,128)}) custom-call(bf16[2048,1024]{1,0:T(8,128)(2,1)} %x_hbm.1, bf16[1024,512]{1,0:T(8,128)(2,1)} %w1_hbm.1, bf16[512,1024]{1,0:T(8,128)(2,1)} %w2_hbm.1, bf16[12,1024]{1,0:T(8,128)(2,1)} %reshape.12.ht_ref, s32[4,2048]{1,0:T(4,128)} %lab_ref.1), custom_call_target="tpu_custom_call" | custom-call | tf_op jit(solution)/shard_map/trunk/pallas_call | solution.py:483
  171.8 1.8 %write.1 = (f32[1,4]{1,0:T(1,128)}, f32[128,512]{1,0:T(8,128)}, f32[64,1024]{1,0:T(8,128)}) custom-call(f32[8,128]{1,0:T(8,128)} %get-tuple-element.9.a_ref, f32[128,512]{1,0:T(8,128)} %get-tuple-element.10.g1_ref, f32[64,1024]{1,0:T(8,128)} %get-tuple-element.11.g2_ref), custom_call_target="tpu_custom_call" | custom-call | tf_op jit(solution)/shard_map/write/pallas_call | solution.py:510

commit v3 on v2

--- a/solution.py
+++ b/solution.py
@@ -33,7 +33,7 @@
         dest = lax.rem(self.me + self.n + sign * dist, self.n)
         target = lax.rem(self.me + self.n + sign, self.n)
         return pltpu.make_async_remote_copy(
-            src_ref=self.chunk(dest, half, sign * dist % self.n), dst_ref=self.recv.at[d, i],
+            src_ref=self.chunk(dest, half, sign * dist % self.n), dst_ref=self.recv(d, i),
             send_sem=self.send_sem.at[d, i], recv_sem=self.recv_sem.at[d, i],
             device_id=self.peer(target), device_id_type=pl.DeviceIdType.MESH)
 
@@ -51,7 +51,7 @@
             half = d if far else 1 - d
             self.copy(d, i).wait_recv()
             dest = lax.rem(self.me + self.n + sign * (dist - 1), self.n)
-            self.add(dest, half, sign * (dist - 1) % self.n, self.recv.at[d, i])
+            self.add(dest, half, sign * (dist - 1) % self.n, self.recv(d, i))
             if i + 2 <= self.n - 2:
                 self.send(d, i + 2)
 
@@ -64,9 +64,9 @@
 def trunk_kernel(nz, ny, nx, n_total, x_hbm, w1_hbm, w2_hbm, ht_ref, lab_ref,
                  a_out, g1_out, g2_out,
                  xd, w1_v, w2_v, ht_v, hb, gg2, gg1, ut_v, sl_v, xt_v, da, ecol,
-                 rya, ryb, ryc, rz1, rz2, ry2, agy, agz, zrow, logit,
+                 rya, ryb, ryc, rz1, rz2, ry2, agm, zrow, logit,
                  d1, d2, r1, r2, gram_d, gram_m, m1, m2,
-                 sya, vya, syb, vyb, syc, vyc, sz1, vz1, sz2, vz2, sy2, vy2, say, vay, saz, vaz,
+                 sya, vya, syb, vyb, syc, vyc, sz1, vz1, sz2, vz2, sy2, vy2, sam, vam,
                  w_sem, x_sem, sd, vd, sx, vx, sgd, vgd, sgm, vgm, o_sem):
     me = lax.axis_index('model')
     dat = lax.axis_index('data')
@@ -76,6 +76,7 @@
     rows, n_dim = gg2.shape[2], gg2.shape[3]
     n_tok, n_ffn = sl_v.shape
     n_task = gg2.shape[0] // CORES
+    n_class = ht_ref.shape[0]
     half_rows = rows // 2
     c1 = rya.shape[4]
     blk = ny * rows
@@ -155,16 +156,19 @@
     def add_y2(dest, half, off, buf):
         gg2[own, dest, hs(half), right] += buf[...]
 
+    def landing(buf):
+        return lambda d, i: buf.at[d, i]
+
     rings = {
-        'z1': Ring(nz, z, peer_z, lambda t, h, o: gg2.at[slot(o), y, hs(h), left], rz1, sz1, vz1, add_z1),
-        'z2': Ring(nz, z, peer_z, lambda t, h, o: gg2.at[slot(o), :, hs(h), right], rz2, sz2, vz2, add_z2),
-        'y2': Ring(ny, y, peer_y, lambda t, h, o: gg2.at[own, t, hs(h), right], ry2, sy2, vy2, add_y2),
+        'z1': Ring(nz, z, peer_z, lambda t, h, o: gg2.at[slot(o), y, hs(h), left], landing(rz1), sz1, vz1, add_z1),
+        'z2': Ring(nz, z, peer_z, lambda t, h, o: gg2.at[slot(o), :, hs(h), right], landing(rz2), sz2, vz2, add_z2),
+        'y2': Ring(ny, y, peer_y, lambda t, h, o: gg2.at[own, t, hs(h), right], landing(ry2), sy2, vy2, add_y2),
     }
     first = 0
     for name, recv, send_sem, recv_sem in (('ya', rya, sya, vya), ('yb', ryb, syb, vyb), ('yc', ryc, syc, vyc)):
         group = pl.ds(first, recv.shape[2])
         rings[name] = Ring(ny, y, peer_y, lambda t, h, o, group=group: gg2.at[group, t, hs(h), left],
-                           recv, send_sem, recv_sem, add_y1(first))
+                           landing(recv), send_sem, recv_sem, add_y1(first))
         first += recv.shape[2]
 
     scale = np.float32(np.sqrt(2.0 / np.pi))
@@ -199,17 +203,17 @@
         xt_v[:, at] = xd[at, :].T
         return 0
     lax.fori_loop(0, nz, flip, 0)
-    n_head = ht_ref.shape[0]
     ht_v[...] = jnp.zeros_like(ht_v)
-    ht_v[0:n_head, :] = ht_ref[...]
-    for k in range(n_head):
-        hb[k] = jnp.broadcast_to(ht_v[k:k + 1, :].astype(F32), (8, n_dim))
+    for c in range(n_class):
+        ht_v[4 * c:4 * c + n_task, :] = ht_ref[c].astype(F32)
+        for t in range(n_task):
+            hb[4 * c + t] = jnp.broadcast_to(ht_ref[c, t:t + 1, :].astype(F32), (8, n_dim))
 
     order = [
         ('z2', 0), ('ya', 0), ('z2', 1), ('z2', 2), ('ya', 1), ('z2', 3), ('ya', 2), ('z2', 4), ('yb', 0), ('z1', 0),
         ('yb', 1), ('z2', 5), ('yb', 2), ('z1', 1), ('z1', 2), ('z2', 6), ('yc', 0), ('yc', 1), ('y2', 0), ('y2', 1),
         ('yc', 2), ('z1', 3), ('z1', 4), ('y2', 2), ('z1', 5), ('z1', 6)]
-    begins = {('ya', 0): 'yb', ('ya', 2): 'z1', ('yb', 0): 'yc', ('z2', 6): 'y2'}
+    begins = {('ya', 0): 'yb', ('ya', 2): 'z1', ('yb', 0): 'yc', ('yc', 0): 'y2'}
     for event in order:
         name, i = event
         rings[name].step(i)
@@ -219,19 +223,22 @@
 
     mine = pl.ds(pl.multiple_of(me * rows, rows), rows)
     zrow[...] = (xd[mine, :].astype(F32) + gg2[own, y]).astype(BF16)
-    logit[...] = lax.dot_general(ht_v[...], zrow[...], (((1,), (1,)), ((), ())), preferred_element_type=F32)
-    l0, l1, l2 = logit[0:4, :], logit[4:8, :], logit[8:12, :]
-    top = jnp.maximum(jnp.maximum(l0, l1), l2)
-    e0, e1, e2 = jnp.exp(l0 - top), jnp.exp(l1 - top), jnp.exp(l2 - top)
-    total = e0 + e1 + e2
+    logit[...] = lax.dot_general(ht_v[...].astype(BF16), zrow[...], (((1,), (1,)), ((), ())), preferred_element_type=F32)
     per = 128 // rows
     wide = lab_ref[:, pl.ds(pl.multiple_of(lax.div(me, per) * 128, 128), 128)]
     lab = wide[:, :rows]
     for k in range(1, per):
         lab = jnp.where(lax.rem(me, per) == k, wide[:, k * rows:(k + 1) * rows], lab)
-    agy[y] = jnp.zeros((16, 128), F32)
-    for c, e in enumerate((e0, e1, e2)):
-        agy[y, 4 * c:4 * c + 4, 0:rows] = (e / total - jnp.where(lab == c, 1.0, 0.0)) / n_total
+    agm[me] = jnp.zeros((8, 128), F32)
+    for t in range(n_task):
+        ls = [logit[4 * c + t:4 * c + t + 1, :] for c in range(n_class)]
+        top = functools.reduce(jnp.maximum, ls)
+        es = [jnp.exp(v - top) for v in ls]
+        total = functools.reduce(jnp.add, es)
+        for c in range(n_class):
+            row, first = 2 * c + t // 2, t % 2 * rows
+            agm[me, row:row + 1, first:first + rows] = (
+                es[c] / total - jnp.where(lab[t:t + 1, :] == c, 1.0, 0.0)) / n_total
 
     sends = []
 
@@ -252,44 +259,37 @@
             if use:
                 use(src)
 
-    exchange(ny, y, peer_y, lambda p: agy.at[p], say, vay)
-    low = lax.broadcasted_iota(jnp.int32, (16, 128), 1)
-    for q in range(ny // per):
-        tile = agy[q * per]
-        for k in range(1, per):
-            tile = jnp.where(low >= k * rows, pltpu.roll(agy[q * per + k], k * rows, 1), tile)
-        agz[z, :, q * 128:(q + 1) * 128] = tile
-
     def turn(k):
-        ecol[pl.ds(pl.multiple_of(k * blk, blk), blk), :] = agz[k].T
-
-    exchange(nz, z, peer_z, lambda p: agz.at[p], saz, vaz, turn)
+        ecol[k] = agm[k].T
+
+    exchange(n_model, me, peer_m, lambda p: agm.at[p], sam, vam, turn)
     for ring in rings.values():
         ring.finish()
 
-    rb = 64
-
-    def make_dz(t):
+    def make_dz(t, cols):
         def body(i, _):
-            at = pl.ds(pl.multiple_of(i * rb, rb), rb)
-            es = [jnp.broadcast_to(ecol[at, 4 * c + t:4 * c + t + 1], (rb, 128)) for c in range(3)]
-            for j in range(0, n_dim, 128):
-                hs3 = [jnp.concatenate([hb[4 * c + t, :, j:j + 128]] * (rb // 8), axis=0) for c in range(3)]
-                xd[at, j:j + 128] = (es[0] * hs3[0] + es[1] * hs3[1] + es[2] * hs3[2]).astype(BF16)
-            return 0
-        lax.fori_loop(0, n_tok // rb, body, 0, unroll=4)
+            at = pl.ds(pl.multiple_of(i * rows, rows), rows)
+            first = t % 2 * rows
+            es = [jnp.broadcast_to(ecol[i, first:first + rows, 2 * c + t // 2:2 * c + t // 2 + 1], (rows, 128))
+                  for c in range(n_class)]
+            for j in range(cols[0], cols[1], 128):
+                parts = [es[c] * jnp.concatenate([hb[4 * c + t, :, j:j + 128]] * (rows // 8), axis=0)
+                         for c in range(n_class)]
+                xd[at, j:j + 128] = functools.reduce(jnp.add, parts).astype(BF16)
+            return 0
+        lax.fori_loop(0, n_model, body, 0, unroll=4)
 
     tile = 256
     q1 = gg1.shape[2]
 
-    def make_g2(t):
+    def make_g2(t, cols):
         def body(i, _):
             at = pl.ds(pl.multiple_of(i * tile, tile), tile)
             out = jnp.dot(ut_v[...], xd[:, at], preferred_element_type=F32).reshape(nx, CORES, rows, tile)
             for c in range(CORES):
                 gg2[CORES * t + c, :, :, at] = out[:, c]
             return 0
-        lax.fori_loop(0, n_dim // tile, body, 0)
+        lax.fori_loop(cols[0] // tile, cols[1] // tile, body, 0)
 
     def make_da():
         def body(i, _):
@@ -312,36 +312,47 @@
             return 0
         lax.fori_loop(0, n_ffn // tile, body, 0)
 
-    n_stage = 2 * n_task
-    sets = ((gg2, d2, r2), (gg1, d1, r1))
+    all1, all2 = (0, n_ffn), (0, n_dim)
+    stages = [(2, 0, (0, n_dim // 2)), (2, 0, (n_dim // 2, n_dim)), (1, 0, all1)]
+    for t in range(1, n_task):
+        stages += [(2, t, all2), (1, t, all1)]
+    n_stage = len(stages)
+    sets = {2: (gg2, d2, r2), 1: (gg1, d1, r1)}
+
+    def columns(s):
+        first, last = stages[s][2]
+        return pl.ds(first, last - first)
 
     def swap(s):
-        g, buf, _ = sets[s % 2]
-        t = s // 2
+        g, buf, _ = sets[stages[s][0]]
+        t = stages[s][1]
         return pltpu.make_async_remote_copy(
-            src_ref=g.at[CORES * t + 1 - core], dst_ref=buf.at[t], send_sem=sd.at[s], recv_sem=vd.at[s],
-            device_id=other, device_id_type=pl.DeviceIdType.MESH)
+            src_ref=g.at[CORES * t + 1 - core, :, :, columns(s)], dst_ref=buf.at[t, :, :, columns(s)],
+            send_sem=sd.at[s], recv_sem=vd.at[s], device_id=other, device_id_type=pl.DeviceIdType.MESH)
 
     def ring_of(s):
-        g, _, r = sets[s % 2]
-        t = s // 2
+        g, _, r = sets[stages[s][0]]
+        t = stages[s][1]
         half = g.shape[2] // 2
 
         def chunk(dest, h, off):
-            return g.at[CORES * t + core, dest, pl.ds(h * half, half), :]
+            return g.at[CORES * t + core, dest, pl.ds(h * half, half), columns(s)]
 
         def add(dest, h, off, buf):
-            g[CORES * t + core, dest, pl.ds(h * half, half), :] += buf[...]
-
-        return Ring(nx, x, peer_x, chunk, r.at[t], sx.at[s], vx.at[s], add)
+            g[CORES * t + core, dest, pl.ds(h * half, half), columns(s)] += buf[...]
+
+        def into(d, i):
+            return r.at[t, d, i, :, columns(s)]
+
+        return Ring(nx, x, peer_x, chunk, into, sx.at[s], vx.at[s], add)
 
     def launch(s):
-        g, buf, _ = sets[s % 2]
-        t = s // 2
+        g, buf, _ = sets[stages[s][0]]
+        t = stages[s][1]
         swap(s).wait_recv()
 
         def body(k, _):
-            g[CORES * t + core, k] += buf[t, k]
+            g[CORES * t + core, k, :, columns(s)] += buf[t, k, :, columns(s)]
             return 0
         lax.fori_loop(0, nx, body, 0)
         if s >= 2:
@@ -350,13 +361,15 @@
         ring_of(s).begin(1)
 
     for s in range(n_stage):
-        t = s // 2
-        if s % 2 == 0:
-            make_dz(t)
-            if s >= 1:
+        which, t, cols = stages[s]
+        if which == 2:
+            make_dz(t, cols)
+            if s >= 2:
                 launch(s - 1)
-            make_g2(t)
+            make_g2(t, cols)
         else:
+            if s == 2:
+                launch(0)
             make_da()
             launch(s - 1)
             make_g1(t)
@@ -473,12 +486,12 @@
         c2 = n_dim - c1
         f1 = n_dim // n_data
         f2 = n_ffn // n_data
-        heads = jnp.transpose(task_heads, (2, 0, 1)).reshape(n_class * n_task, n_dim)
+        heads = jnp.transpose(task_heads, (2, 0, 1))
         vm = pl.BlockSpec(memory_space=pltpu.VMEM)
         hbm = pl.BlockSpec(memory_space=pl.ANY)
         dma = pltpu.SemaphoreType.DMA
         outs = [jax.ShapeDtypeStruct((f1, n_ffn), F32), jax.ShapeDtypeStruct((f2, n_dim), F32)]
-        stages = 2 * n_task
+        stages = 2 * n_task + 1
 
         results = pl.pallas_call(
             functools.partial(trunk_kernel, nz, ny, nx, n_tok * n_data),
@@ -486,14 +499,14 @@
             in_specs=[hbm] * 3 + [vm] * 2, out_specs=[vm, hbm, hbm],
             scratch_shapes=[
                 pltpu.VMEM((n_tok, n_dim), BF16), pltpu.VMEM((n_dim, n_ffn), BF16), pltpu.VMEM((n_ffn, n_dim), BF16),
-                pltpu.VMEM((16, n_dim), BF16), pltpu.VMEM((n_class * n_task, 8, n_dim), F32),
+                pltpu.VMEM((16, n_dim), F32), pltpu.VMEM((n_class * n_task, 8, n_dim), F32),
                 pltpu.VMEM((CORES * n_task, nx, f2, n_dim), F32), pltpu.VMEM((CORES * n_task, nx, f1, n_ffn), F32),
                 pltpu.VMEM((n_ffn, n_tok), BF16), pltpu.VMEM((n_tok, n_ffn), F32), pltpu.VMEM((n_dim, n_tok), BF16),
-                pltpu.VMEM((n_tok, n_ffn), BF16), pltpu.VMEM((n_tok, 16), F32),
+                pltpu.VMEM((n_tok, n_ffn), BF16), pltpu.VMEM((n_model, 128, 8), F32),
                 pltpu.VMEM((2, ny - 1, 3, hr, c1), F32), pltpu.VMEM((2, ny - 1, nz - 6, hr, c1), F32),
                 pltpu.VMEM((2, ny - 1, 3, hr, c1), F32), pltpu.VMEM((2, nz - 1, hr, c1), F32),
                 pltpu.VMEM((2, nz - 1, ny, hr, c2), F32), pltpu.VMEM((2, ny - 1, hr, c2), F32),
-                pltpu.VMEM((ny, 16, 128), F32), pltpu.VMEM((nz, 16, ny * rows), F32),
+                pltpu.VMEM((n_model, 8, 128), F32),
                 pltpu.VMEM((rows, n_dim), BF16), pltpu.VMEM((16, rows), F32),
                 pltpu.VMEM((n_task, nx, f1, n_ffn), F32), pltpu.VMEM((n_task, nx, f2, n_dim), F32),
                 pltpu.VMEM((n_task, 2, nx - 1, f1 // 2, n_ffn), F32), pltpu.VMEM((n_task, 2, nx - 1, f2 // 2, n_dim), F32),
@@ -501,7 +514,7 @@
                 pltpu.VMEM((f1, n_ffn), F32), pltpu.VMEM((f2, n_dim), F32),
                 *[dma((2, ny - 1))] * 6, dma((2, nz - 1)), dma((2, nz - 1)),
                 dma((2, nz - 1)), dma((2, nz - 1)), dma((2, ny - 1)), dma((2, ny - 1)),
-                dma((ny,)), dma((ny,)), dma((nz,)), dma((nz,)),
+                dma((n_model,)), dma((n_model,)),
                 dma((2,)), dma((nz,)), dma((stages,)), dma((stages,)), dma((stages, 2, nx - 1)), dma((stages, 2, nx - 1)),
                 dma((n_data,)), dma((n_data,)), dma((n_model,)), dma((n_model,)), dma((2,))],
             compiler_params=pltpu.CompilerParams(collective_id=0, has_side_effects=True, vmem_limit_bytes=VMEM_LIMIT),

time: 174 us -> 172 us (0.989)
  no operation moved by 1% of the time
where the time goes in v3:
time: 172 us
  Pallas kernels  171 us (99%)
    pallas_call x1, Pallas kernels, local_step(): pl.pallas_call(functools.partial(trunk_kernel, nz, ny, nx, n_tok * n_data...  169 us

profile of v3, /device:TPU:1, one launch (start us, length us, event | category | flops | bytes accessed | tf_op | source)
XLA Modules:
  0.0 171.7 jit_solution(9956698947176630873)
XLA Ops:
  0.6 169.2 %trunk.1 = (f32[8,128]{1,0:T(8,128)}, f32[128,512]{1,0:T(8,128)}, f32[64,1024]{1,0:T(8,128)}) custom-call(bf16[2048,1024]{1,0:T(8,128)(2,1)} %x_hbm.1, bf16[1024,512]{1,0:T(8,128)(2,1)} %w1_hbm.1, bf16[512,1024]{1,0:T(8,128)(2,1)} %w2_hbm.1, bf16[3,4,1024]{2,1,0:T(4,128)(2,1)} %bitcast.2, s32[4,2048]{1,0:T(4,128)} %lab_ref.1), custom_call_target="tpu_custom_call" | custom-call | tf_op jit(solution)/shard_map/trunk/pallas_call | solution.py:496
  169.9 1.8 %write.1 = (f32[1,4]{1,0:T(1,128)}, f32[128,512]{1,0:T(8,128)}, f32[64,1024]{1,0:T(8,128)}) custom-call(f32[8,128]{1,0:T(8,128)} %get-tuple-element.9.a_ref, f32[128,512]{1,0:T(8,128)} %get-tuple-element.10.g1_ref, f32[64,1024]{1,0:T(8,128)} %get-tuple-element.11.g2_ref), custom_call_target="tpu_custom_call" | custom-call | tf_op jit(solution)/shard_map/write/pallas_call | solution.py:523

commit v4 on v3

--- a/solution.py
+++ b/solution.py
@@ -34,7 +34,7 @@
         target = lax.rem(self.me + self.n + sign, self.n)
         return pltpu.make_async_remote_copy(
             src_ref=self.chunk(dest, half, sign * dist % self.n), dst_ref=self.recv(d, i),
-            send_sem=self.send_sem.at[d, i], recv_sem=self.recv_sem.at[d, i],
+            send_sem=self.send_sem, recv_sem=self.recv_sem.at[d, i],
             device_id=self.peer(target), device_id_type=pl.DeviceIdType.MESH)
 
     def send(self, d, i):
@@ -55,10 +55,11 @@
             if i + 2 <= self.n - 2:
                 self.send(d, i + 2)
 
-    def finish(self):
-        for i in range(self.n - 1):
-            for d in (0, 1):
-                self.copy(d, i).wait_send()
+
+def sent(buf, send_sem, recv_sem, peer):
+    pltpu.make_async_remote_copy(
+        src_ref=buf, dst_ref=buf, send_sem=send_sem, recv_sem=recv_sem,
+        device_id=peer, device_id_type=pl.DeviceIdType.MESH).wait_send()
 
 
 def trunk_kernel(nz, ny, nx, n_total, x_hbm, w1_hbm, w2_hbm, ht_ref, lab_ref,
@@ -160,15 +161,15 @@
         return lambda d, i: buf.at[d, i]
 
     rings = {
-        'z1': Ring(nz, z, peer_z, lambda t, h, o: gg2.at[slot(o), y, hs(h), left], landing(rz1), sz1, vz1, add_z1),
-        'z2': Ring(nz, z, peer_z, lambda t, h, o: gg2.at[slot(o), :, hs(h), right], landing(rz2), sz2, vz2, add_z2),
-        'y2': Ring(ny, y, peer_y, lambda t, h, o: gg2.at[own, t, hs(h), right], landing(ry2), sy2, vy2, add_y2),
+        'z1': Ring(nz, z, peer_z, lambda t, h, o: gg2.at[slot(o), y, hs(h), left], landing(rz1), sz1.at[0], vz1, add_z1),
+        'z2': Ring(nz, z, peer_z, lambda t, h, o: gg2.at[slot(o), :, hs(h), right], landing(rz2), sz2.at[0], vz2, add_z2),
+        'y2': Ring(ny, y, peer_y, lambda t, h, o: gg2.at[own, t, hs(h), right], landing(ry2), sy2.at[0], vy2, add_y2),
     }
     first = 0
     for name, recv, send_sem, recv_sem in (('ya', rya, sya, vya), ('yb', ryb, syb, vyb), ('yc', ryc, syc, vyc)):
         group = pl.ds(first, recv.shape[2])
         rings[name] = Ring(ny, y, peer_y, lambda t, h, o, group=group: gg2.at[group, t, hs(h), left],
-                           landing(recv), send_sem, recv_sem, add_y1(first))
+                           landing(recv), send_sem.at[0], recv_sem, add_y1(first))
         first += recv.shape[2]
 
     scale = np.float32(np.sqrt(2.0 / np.pi))
@@ -211,8 +212,8 @@
 
     order = [
         ('z2', 0), ('ya', 0), ('z2', 1), ('z2', 2), ('ya', 1), ('z2', 3), ('ya', 2), ('z2', 4), ('yb', 0), ('z1', 0),
-        ('yb', 1), ('z2', 5), ('yb', 2), ('z1', 1), ('z1', 2), ('z2', 6), ('yc', 0), ('yc', 1), ('y2', 0), ('y2', 1),
-        ('yc', 2), ('z1', 3), ('z1', 4), ('y2', 2), ('z1', 5), ('z1', 6)]
+        ('yb', 1), ('z2', 5), ('yb', 2), ('z1', 1), ('z1', 2), ('z2', 6), ('yc', 0), ('yc', 1), ('yc', 2), ('z1', 3),
+        ('z1', 4), ('y2', 0), ('y2', 1), ('z1', 5), ('y2', 2), ('z1', 6)]
     begins = {('ya', 0): 'yb', ('ya', 2): 'z1', ('yb', 0): 'yc', ('yc', 0): 'y2'}
     for event in order:
         name, i = event
@@ -240,31 +241,26 @@
             agm[me, row:row + 1, first:first + rows] = (
                 es[c] / total - jnp.where(lab[t:t + 1, :] == c, 1.0, 0.0)) / n_total
 
-    sends = []
-
-    def exchange(n, pos, peer, view, send_sem, recv_sem, use=None):
+    def exchange(n, pos, peer, buf, send_sem, recv_sem, use):
         def copy(k, src):
             return pltpu.make_async_remote_copy(
-                src_ref=view(pos), dst_ref=view(src), send_sem=send_sem.at[k], recv_sem=recv_sem.at[k],
+                src_ref=buf.at[pos], dst_ref=buf.at[src], send_sem=send_sem.at[0], recv_sem=recv_sem.at[k],
                 device_id=peer(lax.rem(pos + k, n)), device_id_type=pl.DeviceIdType.MESH)
         for k in range(1, n):
-            cp = copy(k, pos)
-            cp.start()
-            sends.append(cp)
-        if use:
-            use(pos)
+            copy(k, pos).start()
+        use(pos)
         for k in range(1, n):
             src = lax.rem(pos + n - k, n)
             copy(k, src).wait_recv()
-            if use:
-                use(src)
+            use(src)
 
     def turn(k):
         ecol[k] = agm[k].T
 
-    exchange(n_model, me, peer_m, lambda p: agm.at[p], sam, vam, turn)
-    for ring in rings.values():
-        ring.finish()
+    exchange(n_model, me, peer_m, agm, sam, vam, turn)
+    for buf, send_sem, recv_sem in ((rya, sya, vya), (ryb, syb, vyb), (ryc, syc, vyc), (rz1, sz1, vz1), (rz2, sz2, vz2),
+                                    (ry2, sy2, vy2)):
+        sent(buf, send_sem.at[0], recv_sem.at[0, 0], other)
 
     def make_dz(t, cols):
         def body(i, _):
@@ -328,7 +324,7 @@
         t = stages[s][1]
         return pltpu.make_async_remote_copy(
             src_ref=g.at[CORES * t + 1 - core, :, :, columns(s)], dst_ref=buf.at[t, :, :, columns(s)],
-            send_sem=sd.at[s], recv_sem=vd.at[s], device_id=other, device_id_type=pl.DeviceIdType.MESH)
+            send_sem=sd.at[stages[s][0] - 1], recv_sem=vd.at[s], device_id=other, device_id_type=pl.DeviceIdType.MESH)
 
     def ring_of(s):
         g, _, r = sets[stages[s][0]]
@@ -344,7 +340,7 @@
         def into(d, i):
             return r.at[t, d, i, :, columns(s)]
 
-        return Ring(nx, x, peer_x, chunk, into, sx.at[s], vx.at[s], add)
+        return Ring(nx, x, peer_x, chunk, into, sx.at[stages[s][0] - 1], vx.at[s], add)
 
     def launch(s):
         g, buf, _ = sets[stages[s][0]]
@@ -355,7 +351,9 @@
             g[CORES * t + core, k, :, columns(s)] += buf[t, k, :, columns(s)]
             return 0
         lax.fori_loop(0, nx, body, 0)
-        if s >= 2:
+        if s == 2:
+            ring_of(1).step(0)
+        if s >= 4:
             ring_of(s - 2).step(0)
         ring_of(s).begin(0)
         ring_of(s).begin(1)
@@ -373,6 +371,8 @@
             make_da()
             launch(s - 1)
             make_g1(t)
+            if s == 2:
+                ring_of(0).step(0)
         swap(s).start()
     launch(n_stage - 1)
     for s in (n_stage - 2, n_stage - 1):
@@ -404,7 +404,17 @@
 
     def all_sum(n, pos, peer, buf, send_sem, recv_sem, val):
         buf[pos, 0:1, :] = val
-        exchange(n, pos, peer, lambda p: buf.at[p, pl.ds(0, 1), :], send_sem, recv_sem)
+        for k in range(1, n):
+            pltpu.make_async_remote_copy(
+                src_ref=buf.at[pos, pl.ds(0, 1), :], dst_ref=buf.at[pos, pl.ds(0, 1), :],
+                send_sem=send_sem.at[0], recv_sem=recv_sem.at[k],
+                device_id=peer(lax.rem(pos + k, n)), device_id_type=pl.DeviceIdType.MESH).start()
+        for k in range(1, n):
+            src = lax.rem(pos + n - k, n)
+            pltpu.make_async_remote_copy(
+                src_ref=buf.at[src, pl.ds(0, 1), :], dst_ref=buf.at[src, pl.ds(0, 1), :],
+                send_sem=send_sem.at[0], recv_sem=recv_sem.at[k],
+                device_id=peer(src), device_id_type=pl.DeviceIdType.MESH).wait_recv()
         out = buf[0, 0:1, :]
         for k in range(1, n):
             out = out + buf[k, 0:1, :]
@@ -413,30 +423,25 @@
     part = all_sum(nd, dat, peer_d, gram_d, sgd, vgd, part)
     part = all_sum(n_model, me, peer_m, gram_m, sgm, vgm, part)
 
-    row_id = lax.broadcasted_iota(jnp.int32, (8, 128), 0)
-    col_id = lax.broadcasted_iota(jnp.int32, (8, 128), 1)
-    eye = row_id == col_id
-    wide8 = jnp.broadcast_to(part, (8, 128))
-    gram = jnp.zeros((8, 128), F32)
+    gram = [[jnp.broadcast_to(part[:, n_task * i + j:n_task * i + j + 1], (1, 128)) for j in range(n_task)]
+            for i in range(n_task)]
+    trace_scale = functools.reduce(jnp.add, [gram[i][i] for i in range(n_task)]) / n_task
+
+    def eg(i, ws):
+        ups = []
+        for t in range(n_task):
+            prod = functools.reduce(jnp.add, [gram[t][j] * ws[j] for j in range(n_task)])
+            ups.append(ws[t] * jnp.exp(-prod / trace_scale))
+        total = functools.reduce(jnp.add, ups)
+        return tuple(up / total for up in ups)
+
+    ws = tuple(jnp.full((1, 128), 1.0 / n_task, F32) for _ in range(n_task))
+    ws = lax.fori_loop(0, STEPS, eg, ws)
+    weights = jnp.zeros((1, 128), F32)
     for t in range(n_task):
-        moved = pltpu.roll(wide8, 128 - n_task * t, 1) if t else wide8
-        gram = jnp.where((row_id == t) & (col_id < n_task), moved, gram)
-    trace = jnp.sum(jnp.sum(jnp.where(eye, gram, 0.0), axis=1, keepdims=True), axis=0, keepdims=True)
-    trace_scale = trace / n_task
-    wrow = jnp.where(col_id < n_task, 1.0 / n_task, 0.0).astype(F32)
-    wcol = jnp.where(row_id < n_task, 1.0 / n_task, 0.0).astype(F32)
-
-    def eg(i, carry):
-        wrow, wcol = carry
-        prod = jnp.sum(gram * wrow, axis=1, keepdims=True)
-        up = wcol * jnp.exp(-prod / trace_scale)
-        new = up / jnp.sum(up, axis=0, keepdims=True)
-        return jnp.sum(jnp.where(eye, new, 0.0), axis=0, keepdims=True) + jnp.zeros_like(wrow), new
-
-    wrow, wcol = lax.fori_loop(0, STEPS, eg, (wrow, wcol))
-    a_out[...] = wrow
+        weights = jnp.where(lane == t, ws[t], weights)
+    a_out[0:1, :] = weights
     writes = []
-    ws = [wcol[t:t + 1, :] for t in range(n_task)]
 
     def mix(g, out):
         width = g.shape[3]
@@ -457,11 +462,12 @@
 
     for c in writes:
         c.wait()
-    for c in sends:
-        c.wait_send()
-    for s in range(n_stage):
-        swap(s).wait_send()
-        ring_of(s).finish()
+    sent(agm.at[pl.ds(0, n_model - 1)], sam.at[0], vam.at[0], other)
+    sent(gram_d.at[pl.ds(0, nd - 1), pl.ds(0, 1), :], sgd.at[0], vgd.at[0], other)
+    sent(gram_m.at[pl.ds(0, n_model - 1), pl.ds(0, 1), :], sgm.at[0], vgm.at[0], other)
+    for k, (d, r) in enumerate(((d1, r1), (d2, r2))):
+        sent(d, sd.at[k], vd.at[0], other)
+        sent(r, sx.at[k], vx.at[0, 0, 0], other)
 
 
 def write_kernel(a_ref, g1_ref, g2_ref, a_out, g1_out, g2_out):
@@ -512,11 +518,11 @@
                 pltpu.VMEM((n_task, 2, nx - 1, f1 // 2, n_ffn), F32), pltpu.VMEM((n_task, 2, nx - 1, f2 // 2, n_dim), F32),
                 pltpu.VMEM((n_data, 8, 128), F32), pltpu.VMEM((n_model, 8, 128), F32),
                 pltpu.VMEM((f1, n_ffn), F32), pltpu.VMEM((f2, n_dim), F32),
-                *[dma((2, ny - 1))] * 6, dma((2, nz - 1)), dma((2, nz - 1)),
-                dma((2, nz - 1)), dma((2, nz - 1)), dma((2, ny - 1)), dma((2, ny - 1)),
-                dma((n_model,)), dma((n_model,)),
-                dma((2,)), dma((nz,)), dma((stages,)), dma((stages,)), dma((stages, 2, nx - 1)), dma((stages, 2, nx - 1)),
-                dma((n_data,)), dma((n_data,)), dma((n_model,)), dma((n_model,)), dma((2,))],
+                *[dma((1,)), dma((2, ny - 1))] * 3, dma((1,)), dma((2, nz - 1)),
+                dma((1,)), dma((2, nz - 1)), dma((1,)), dma((2, ny - 1)),
+                dma((1,)), dma((n_model,)),
+                dma((2,)), dma((nz,)), dma((2,)), dma((stages,)), dma((2,)), dma((stages, 2, nx - 1)),
+                dma((1,)), dma((n_data,)), dma((1,)), dma((n_model,)), dma((2,))],
             compiler_params=pltpu.CompilerParams(collective_id=0, has_side_effects=True, vmem_limit_bytes=VMEM_LIMIT),
             name='trunk',
         )(tokens, w_up, w_down, heads, labels)

time: 172 us -> 167 us (0.971)
  Pallas kernels: 171 us -> 166 us
    pallas_call x1, Pallas kernels: 169 us -> 164 us  [local_step(): pl.pallas_call(functools.partial(trunk_kernel, nz, ny, nx, n_tok * n_data...]
where the time goes in v4:
time: 167 us
  Pallas kernels  166 us (99%)
    pallas_call x1, Pallas kernels, local_step(): pl.pallas_call(functools.partial(trunk_kernel, nz, ny, nx, n_tok * n_data...  164 us

profile of v4, /device:TPU:1, one launch (start us, length us, event | category | flops | bytes accessed | tf_op | source)
XLA Modules:
  0.0 166.7 jit_solution(10624486392688541044)
XLA Ops:
  0.6 164.2 %trunk.1 = (f32[8,128]{1,0:T(8,128)}, f32[128,512]{1,0:T(8,128)}, f32[64,1024]{1,0:T(8,128)}) custom-call(bf16[2048,1024]{1,0:T(8,128)(2,1)} %x_hbm.1, bf16[1024,512]{1,0:T(8,128)(2,1)} %w1_hbm.1, bf16[512,1024]{1,0:T(8,128)(2,1)} %w2_hbm.1, bf16[3,4,1024]{2,1,0:T(4,128)(2,1)} %bitcast.2, s32[4,2048]{1,0:T(4,128)} %lab_ref.1), custom_call_target="tpu_custom_call" | custom-call | tf_op jit(solution)/shard_map/trunk/pallas_call | solution.py:502
  164.9 1.8 %write.1 = (f32[1,4]{1,0:T(1,128)}, f32[128,512]{1,0:T(8,128)}, f32[64,1024]{1,0:T(8,128)}) custom-call(f32[8,128]{1,0:T(8,128)} %get-tuple-element.9.a_ref, f32[128,512]{1,0:T(8,128)} %get-tuple-element.10.g1_ref, f32[64,1024]{1,0:T(8,128)} %get-tuple-element.11.g2_ref), custom_call_target="tpu_custom_call" | custom-call | tf_op jit(solution)/shard_map/write/pallas_call | solution.py:529

commit v5 on v4

--- a/solution.py
+++ b/solution.py
@@ -65,9 +65,9 @@
 def trunk_kernel(nz, ny, nx, n_total, x_hbm, w1_hbm, w2_hbm, ht_ref, lab_ref,
                  a_out, g1_out, g2_out,
                  xd, w1_v, w2_v, ht_v, hb, gg2, gg1, ut_v, sl_v, xt_v, da, ecol,
-                 rya, ryb, ryc, rz1, rz2, ry2, agm, zrow, logit,
+                 rya, ryb, ryc, ryd, rz1, rz2, ry2, agm, zrow, logit,
                  d1, d2, r1, r2, gram_d, gram_m, m1, m2,
-                 sya, vya, syb, vyb, syc, vyc, sz1, vz1, sz2, vz2, sy2, vy2, sam, vam,
+                 sya, vya, syb, vyb, syc, vyc, syd, vyd, sz1, vz1, sz2, vz2, sy2, vy2, sam, vam,
                  w_sem, x_sem, sd, vd, sx, vx, sgd, vgd, sgm, vgm, o_sem):
     me = lax.axis_index('model')
     dat = lax.axis_index('data')
@@ -166,7 +166,7 @@
         'y2': Ring(ny, y, peer_y, lambda t, h, o: gg2.at[own, t, hs(h), right], landing(ry2), sy2.at[0], vy2, add_y2),
     }
     first = 0
-    for name, recv, send_sem, recv_sem in (('ya', rya, sya, vya), ('yb', ryb, syb, vyb), ('yc', ryc, syc, vyc)):
+    for name, recv, send_sem, recv_sem in (('ya', rya, sya, vya), ('yb', ryb, syb, vyb), ('yc', ryc, syc, vyc), ('yd', ryd, syd, vyd)):
         group = pl.ds(first, recv.shape[2])
         rings[name] = Ring(ny, y, peer_y, lambda t, h, o, group=group: gg2.at[group, t, hs(h), left],
                            landing(recv), send_sem.at[0], recv_sem, add_y1(first))
@@ -212,9 +212,9 @@
 
     order = [
         ('z2', 0), ('ya', 0), ('z2', 1), ('z2', 2), ('ya', 1), ('z2', 3), ('ya', 2), ('z2', 4), ('yb', 0), ('z1', 0),
-        ('yb', 1), ('z2', 5), ('yb', 2), ('z1', 1), ('z1', 2), ('z2', 6), ('yc', 0), ('yc', 1), ('yc', 2), ('z1', 3),
-        ('z1', 4), ('y2', 0), ('y2', 1), ('z1', 5), ('y2', 2), ('z1', 6)]
-    begins = {('ya', 0): 'yb', ('ya', 2): 'z1', ('yb', 0): 'yc', ('yc', 0): 'y2'}
+        ('yb', 1), ('z2', 5), ('yb', 2), ('z1', 1), ('yc', 0), ('yc', 1), ('z1', 2), ('z2', 6), ('yc', 2), ('z1', 3),
+        ('z1', 4), ('yd', 0), ('yd', 1), ('yd', 2), ('z1', 5), ('y2', 0), ('y2', 1), ('z1', 6), ('y2', 2)]
+    begins = {('ya', 0): 'yb', ('ya', 2): 'z1', ('yb', 0): 'yc', ('yc', 0): 'yd', ('yd', 0): 'y2'}
     for event in order:
         name, i = event
         rings[name].step(i)
@@ -258,8 +258,8 @@
         ecol[k] = agm[k].T
 
     exchange(n_model, me, peer_m, agm, sam, vam, turn)
-    for buf, send_sem, recv_sem in ((rya, sya, vya), (ryb, syb, vyb), (ryc, syc, vyc), (rz1, sz1, vz1), (rz2, sz2, vz2),
-                                    (ry2, sy2, vy2)):
+    for buf, send_sem, recv_sem in ((rya, sya, vya), (ryb, syb, vyb), (ryc, syc, vyc), (ryd, syd, vyd),
+                                    (rz1, sz1, vz1), (rz2, sz2, vz2), (ry2, sy2, vy2)):
         sent(buf, send_sem.at[0], recv_sem.at[0, 0], other)
 
     def make_dz(t, cols):
@@ -287,13 +287,14 @@
             return 0
         lax.fori_loop(cols[0] // tile, cols[1] // tile, body, 0)
 
-    def make_da():
+    def make_da(part):
         def body(i, _):
             at = pl.ds(pl.multiple_of(i * 2 * tile, 2 * tile), 2 * tile)
             out = lax.dot_general(xd[at, :], w2_v[...], (((1,), (1,)), ((), ())), preferred_element_type=F32)
             da[at, :] = (out * sl_v[at, :]).astype(BF16)
             return 0
-        lax.fori_loop(0, n_tok // (2 * tile), body, 0)
+        n_half = n_tok // (4 * tile)
+        lax.fori_loop(part * n_half, (part + 1) * n_half, body, 0)
 
     def make_g1(t):
         hx = nx // 2
@@ -351,8 +352,6 @@
             g[CORES * t + core, k, :, columns(s)] += buf[t, k, :, columns(s)]
             return 0
         lax.fori_loop(0, nx, body, 0)
-        if s == 2:
-            ring_of(1).step(0)
         if s >= 4:
             ring_of(s - 2).step(0)
         ring_of(s).begin(0)
@@ -362,17 +361,18 @@
         which, t, cols = stages[s]
         if which == 2:
             make_dz(t, cols)
-            if s >= 2:
+            if s >= 1:
                 launch(s - 1)
             make_g2(t, cols)
         else:
+            make_da(0)
+            launch(s - 1)
+            make_da(1)
             if s == 2:
-                launch(0)
-            make_da()
-            launch(s - 1)
+                ring_of(0).step(0)
             make_g1(t)
             if s == 2:
-                ring_of(0).step(0)
+                ring_of(1).step(0)
         swap(s).start()
     launch(n_stage - 1)
     for s in (n_stage - 2, n_stage - 1):
@@ -407,14 +407,12 @@
         for k in range(1, n):
             pltpu.make_async_remote_copy(
                 src_ref=buf.at[pos, pl.ds(0, 1), :], dst_ref=buf.at[pos, pl.ds(0, 1), :],
-                send_sem=send_sem.at[0], recv_sem=recv_sem.at[k],
+                send_sem=send_sem.at[0], recv_sem=recv_sem.at[0],
                 device_id=peer(lax.rem(pos + k, n)), device_id_type=pl.DeviceIdType.MESH).start()
-        for k in range(1, n):
-            src = lax.rem(pos + n - k, n)
-            pltpu.make_async_remote_copy(
-                src_ref=buf.at[src, pl.ds(0, 1), :], dst_ref=buf.at[src, pl.ds(0, 1), :],
-                send_sem=send_sem.at[0], recv_sem=recv_sem.at[k],
-                device_id=peer(src), device_id_type=pl.DeviceIdType.MESH).wait_recv()
+        rest = buf.at[pl.ds(0, n - 1), pl.ds(0, 1), :]
+        pltpu.make_async_remote_copy(
+            src_ref=rest, dst_ref=rest, send_sem=send_sem.at[0], recv_sem=recv_sem.at[0],
+            device_id=other, device_id_type=pl.DeviceIdType.MESH).wait_recv()
         out = buf[0, 0:1, :]
         for k in range(1, n):
             out = out + buf[k, 0:1, :]
@@ -510,7 +508,8 @@
                 pltpu.VMEM((n_ffn, n_tok), BF16), pltpu.VMEM((n_tok, n_ffn), F32), pltpu.VMEM((n_dim, n_tok), BF16),
                 pltpu.VMEM((n_tok, n_ffn), BF16), pltpu.VMEM((n_model, 128, 8), F32),
                 pltpu.VMEM((2, ny - 1, 3, hr, c1), F32), pltpu.VMEM((2, ny - 1, nz - 6, hr, c1), F32),
-                pltpu.VMEM((2, ny - 1, 3, hr, c1), F32), pltpu.VMEM((2, nz - 1, hr, c1), F32),
+                pltpu.VMEM((2, ny - 1, 2, hr, c1), F32), pltpu.VMEM((2, ny - 1, 1, hr, c1), F32),
+                pltpu.VMEM((2, nz - 1, hr, c1), F32),
                 pltpu.VMEM((2, nz - 1, ny, hr, c2), F32), pltpu.VMEM((2, ny - 1, hr, c2), F32),
                 pltpu.VMEM((n_model, 8, 128), F32),
                 pltpu.VMEM((rows, n_dim), BF16), pltpu.VMEM((16, rows), F32),
@@ -518,11 +517,11 @@
                 pltpu.VMEM((n_task, 2, nx - 1, f1 // 2, n_ffn), F32), pltpu.VMEM((n_task, 2, nx - 1, f2 // 2, n_dim), F32),
                 pltpu.VMEM((n_data, 8, 128), F32), pltpu.VMEM((n_model, 8, 128), F32),
                 pltpu.VMEM((f1, n_ffn), F32), pltpu.VMEM((f2, n_dim), F32),
-                *[dma((1,)), dma((2, ny - 1))] * 3, dma((1,)), dma((2, nz - 1)),
+                *[dma((1,)), dma((2, ny - 1))] * 4, dma((1,)), dma((2, nz - 1)),
                 dma((1,)), dma((2, nz - 1)), dma((1,)), dma((2, ny - 1)),
                 dma((1,)), dma((n_model,)),
                 dma((2,)), dma((nz,)), dma((2,)), dma((stages,)), dma((2,)), dma((stages, 2, nx - 1)),
-                dma((1,)), dma((n_data,)), dma((1,)), dma((n_model,)), dma((2,))],
+                dma((1,)), dma((1,)), dma((1,)), dma((1,)), dma((2,))],
             compiler_params=pltpu.CompilerParams(collective_id=0, has_side_effects=True, vmem_limit_bytes=VMEM_LIMIT),
             name='trunk',
         )(tokens, w_up, w_down, heads, labels)

time: 167 us -> 166 us (level)
  no operation moved by 1% of the time
where the time goes in v5:
time: 166 us
  Pallas kernels  165 us (99%)
    pallas_call x1, Pallas kernels, local_step(): pl.pallas_call(functools.partial(trunk_kernel, nz, ny, nx, n_tok * n_data...  163 us

profile of v5, /device:TPU:1, one launch (start us, length us, event | category | flops | bytes accessed | tf_op | source)
XLA Modules:
  0.0 165.6 jit_solution(4320909029671472162)
XLA Ops:
  0.6 163.1 %trunk.1 = (f32[8,128]{1,0:T(8,128)}, f32[128,512]{1,0:T(8,128)}, f32[64,1024]{1,0:T(8,128)}) custom-call(bf16[2048,1024]{1,0:T(8,128)(2,1)} %x_hbm.1, bf16[1024,512]{1,0:T(8,128)(2,1)} %w1_hbm.1, bf16[512,1024]{1,0:T(8,128)(2,1)} %w2_hbm.1, bf16[3,4,1024]{2,1,0:T(4,128)(2,1)} %bitcast.2, s32[4,2048]{1,0:T(4,128)} %lab_ref.1), custom_call_target="tpu_custom_call" | custom-call | tf_op jit(solution)/shard_map/trunk/pallas_call | solution.py:500
  163.8 1.8 %write.1 = (f32[1,4]{1,0:T(1,128)}, f32[128,512]{1,0:T(8,128)}, f32[64,1024]{1,0:T(8,128)}) custom-call(f32[8,128]{1,0:T(8,128)} %get-tuple-element.9.a_ref, f32[128,512]{1,0:T(8,128)} %get-tuple-element.10.g1_ref, f32[64,1024]{1,0:T(8,128)} %get-tuple-element.11.g2_ref), custom_call_target="tpu_custom_call" | custom-call | tf_op jit(solution)/shard_map/write/pallas_call | solution.py:528

commit v6 on v5

--- a/solution.py
+++ b/solution.py
@@ -211,10 +211,10 @@
             hb[4 * c + t] = jnp.broadcast_to(ht_ref[c, t:t + 1, :].astype(F32), (8, n_dim))
 
     order = [
-        ('z2', 0), ('ya', 0), ('z2', 1), ('z2', 2), ('ya', 1), ('z2', 3), ('ya', 2), ('z2', 4), ('yb', 0), ('z1', 0),
-        ('yb', 1), ('z2', 5), ('yb', 2), ('z1', 1), ('yc', 0), ('yc', 1), ('z1', 2), ('z2', 6), ('yc', 2), ('z1', 3),
-        ('z1', 4), ('yd', 0), ('yd', 1), ('yd', 2), ('z1', 5), ('y2', 0), ('y2', 1), ('z1', 6), ('y2', 2)]
-    begins = {('ya', 0): 'yb', ('ya', 2): 'z1', ('yb', 0): 'yc', ('yc', 0): 'yd', ('yd', 0): 'y2'}
+        ('z2', 0), ('ya', 0), ('z2', 1), ('z2', 2), ('ya', 1), ('z2', 3), ('ya', 2), ('yb', 0), ('z2', 4), ('z1', 0),
+        ('yb', 1), ('z2', 5), ('yb', 2), ('z1', 1), ('yc', 0), ('z2', 6), ('yc', 1), ('z1', 2), ('yc', 2), ('z1', 3),
+        ('z1', 4), ('yd', 0), ('yd', 1), ('y2', 0), ('y2', 1), ('yd', 2), ('z1', 5), ('z1', 6), ('y2', 2)]
+    begins = {('ya', 0): 'yb', ('ya', 2): 'z1', ('yb', 0): 'yc', ('yc', 0): 'yd', ('z2', 6): 'y2'}
     for event in order:
         name, i = event
         rings[name].step(i)
@@ -352,7 +352,7 @@
             g[CORES * t + core, k, :, columns(s)] += buf[t, k, :, columns(s)]
             return 0
         lax.fori_loop(0, nx, body, 0)
-        if s >= 4:
+        if s >= 5:
             ring_of(s - 2).step(0)
         ring_of(s).begin(0)
         ring_of(s).begin(1)
@@ -373,6 +373,8 @@
             make_g1(t)
             if s == 2:
                 ring_of(1).step(0)
+            if s == 4:
+                ring_of(2).step(0)
         swap(s).start()
     launch(n_stage - 1)
     for s in (n_stage - 2, n_stage - 1):

time: 166 us -> 163 us (0.982)
  Pallas kernels: 165 us -> 163 us
    pallas_call x1, Pallas kernels: 163 us -> 161 us  [local_step(): pl.pallas_call(functools.partial(trunk_kernel, nz, ny, nx, n_tok * n_data...]
where the time goes in v6:
time: 163 us
  Pallas kernels  163 us (100%)
    pallas_call x1, Pallas kernels, local_step(): pl.pallas_call(functools.partial(trunk_kernel, nz, ny, nx, n_tok * n_data...  161 us

profile of v6, /device:TPU:1, one launch (start us, length us, event | category | flops | bytes accessed | tf_op | source)
XLA Modules:
  0.0 163.1 jit_solution(6055842391398886539)
XLA Ops:
  0.6 160.7 %trunk.1 = (f32[8,128]{1,0:T(8,128)}, f32[128,512]{1,0:T(8,128)}, f32[64,1024]{1,0:T(8,128)}) custom-call(bf16[2048,1024]{1,0:T(8,128)(2,1)} %x_hbm.1, bf16[1024,512]{1,0:T(8,128)(2,1)} %w1_hbm.1, bf16[512,1024]{1,0:T(8,128)(2,1)} %w2_hbm.1, bf16[3,4,1024]{2,1,0:T(4,128)(2,1)} %bitcast.2, s32[4,2048]{1,0:T(4,128)} %lab_ref.1), custom_call_target="tpu_custom_call" | custom-call | tf_op jit(solution)/shard_map/trunk/pallas_call | solution.py:502
  161.3 1.8 %write.1 = (f32[1,4]{1,0:T(1,128)}, f32[128,512]{1,0:T(8,128)}, f32[64,1024]{1,0:T(8,128)}) custom-call(f32[8,128]{1,0:T(8,128)} %get-tuple-element.9.a_ref, f32[128,512]{1,0:T(8,128)} %get-tuple-element.10.g1_ref, f32[64,1024]{1,0:T(8,128)} %get-tuple-element.11.g2_ref), custom_call_target="tpu_custom_call" | custom-call | tf_op jit(solution)/shard_map/write/pallas_call | solution.py:530

commit v7 on v6

--- a/solution.py
+++ b/solution.py
@@ -203,7 +203,6 @@
         at = pl.ds(pl.multiple_of(i * blk, blk), blk)
         xt_v[:, at] = xd[at, :].T
         return 0
-    lax.fori_loop(0, nz, flip, 0)
     ht_v[...] = jnp.zeros_like(ht_v)
     for c in range(n_class):
         ht_v[4 * c:4 * c + n_task, :] = ht_ref[c].astype(F32)
@@ -218,6 +217,8 @@
     for event in order:
         name, i = event
         rings[name].step(i)
+        if event == ('z2', 2):
+            lax.fori_loop(0, nz, flip, 0)
         if event in begins:
             rings[begins[event]].begin(0)
             rings[begins[event]].begin(1)
@@ -296,7 +297,7 @@
         n_half = n_tok // (4 * tile)
         lax.fori_loop(part * n_half, (part + 1) * n_half, body, 0)
 
-    def make_g1(t):
+    def make_g1(t, cols):
         hx = nx // 2
 
         def body(i, _):
@@ -307,10 +308,11 @@
                 for c in range(CORES):
                     gg1[CORES * t + c, k * hx:(k + 1) * hx, :, at] = out[:, c]
             return 0
-        lax.fori_loop(0, n_ffn // tile, body, 0)
+        lax.fori_loop(cols[0] // tile, cols[1] // tile, body, 0)
 
     all1, all2 = (0, n_ffn), (0, n_dim)
-    stages = [(2, 0, (0, n_dim // 2)), (2, 0, (n_dim // 2, n_dim)), (1, 0, all1)]
+    stages = [(2, 0, (0, n_dim // 2)), (2, 0, (n_dim // 2, n_dim)),
+              (1, 0, (0, n_ffn // 2)), (1, 0, (n_ffn // 2, n_ffn))]
     for t in range(1, n_task):
         stages += [(2, t, all2), (1, t, all1)]
     n_stage = len(stages)
@@ -352,7 +354,7 @@
             g[CORES * t + core, k, :, columns(s)] += buf[t, k, :, columns(s)]
             return 0
         lax.fori_loop(0, nx, body, 0)
-        if s >= 5:
+        if s >= 6:
             ring_of(s - 2).step(0)
         ring_of(s).begin(0)
         ring_of(s).begin(1)
@@ -361,27 +363,35 @@
         which, t, cols = stages[s]
         if which == 2:
             make_dz(t, cols)
-            if s >= 1:
+            if s == 1 or s >= 4:
                 launch(s - 1)
             make_g2(t, cols)
+        elif s == 3:
+            make_g1(t, cols)
         else:
             make_da(0)
             launch(s - 1)
             make_da(1)
             if s == 2:
                 ring_of(0).step(0)
-            make_g1(t)
-            if s == 2:
-                ring_of(1).step(0)
-            if s == 4:
-                ring_of(2).step(0)
+            make_g1(t, cols)
         swap(s).start()
+        if s == 2:
+            ring_of(1).step(0)
+        if s == 3:
+            launch(2)
+        if s == 4:
+            ring_of(2).step(0)
+            ring_of(3).step(0)
     launch(n_stage - 1)
     for s in (n_stage - 2, n_stage - 1):
         ring_of(s).step(0)
-    for s in range(n_stage):
+    def settle(s):
         ring_of(s).step(1)
         ring_of(s).step(2)
+
+    for s in range(n_stage - 1):
+        settle(s)
 
     pairs = [(i, j) for i in range(n_task) for j in range(i, n_task)]
 
@@ -397,6 +407,7 @@
 
     accs = tuple(jnp.zeros((8, 128), F32) for _ in pairs)
     accs = fold(gg2, accs)
+    settle(n_stage - 1)
     accs = fold(gg1, accs)
     lane = lax.broadcasted_iota(jnp.int32, (1, 128), 1)
     part = jnp.zeros((1, 128), F32)
@@ -497,7 +508,7 @@
         hbm = pl.BlockSpec(memory_space=pl.ANY)
         dma = pltpu.SemaphoreType.DMA
         outs = [jax.ShapeDtypeStruct((f1, n_ffn), F32), jax.ShapeDtypeStruct((f2, n_dim), F32)]
-        stages = 2 * n_task + 1
+        stages = 2 * n_task + 2
 
         results = pl.pallas_call(
             functools.partial(trunk_kernel, nz, ny, nx, n_tok * n_data),

time: 163 us -> 163 us (level)
  no operation moved by 1% of the time
where the time goes in v7:
time: 163 us
  Pallas kernels  163 us (100%)
    pallas_call x1, Pallas kernels, local_step(): pl.pallas_call(functools.partial(trunk_kernel, nz, ny, nx, n_tok * n_data...  161 us

profile of v7, /device:TPU:1, one launch (start us, length us, event | category | flops | bytes accessed | tf_op | source)
XLA Modules:
  0.0 163.3 jit_solution(3468926353404483105)
XLA Ops:
  0.6 160.8 %trunk.1 = (f32[8,128]{1,0:T(8,128)}, f32[128,512]{1,0:T(8,128)}, f32[64,1024]{1,0:T(8,128)}) custom-call(bf16[2048,1024]{1,0:T(8,128)(2,1)} %x_hbm.1, bf16[1024,512]{1,0:T(8,128)(2,1)} %w1_hbm.1, bf16[512,1024]{1,0:T(8,128)(2,1)} %w2_hbm.1, bf16[3,4,1024]{2,1,0:T(4,128)(2,1)} %bitcast.2, s32[4,2048]{1,0:T(4,128)} %lab_ref.1), custom_call_target="tpu_custom_call" | custom-call | tf_op jit(solution)/shard_map/trunk/pallas_call | solution.py:513
  161.4 1.8 %write.1 = (f32[1,4]{1,0:T(1,128)}, f32[128,512]{1,0:T(8,128)}, f32[64,1024]{1,0:T(8,128)}) custom-call(f32[8,128]{1,0:T(8,128)} %get-tuple-element.9.a_ref, f32[128,512]{1,0:T(8,128)} %get-tuple-element.10.g1_ref, f32[64,1024]{1,0:T(8,128)} %get-tuple-element.11.g2_ref), custom_call_target="tpu_custom_call" | custom-call | tf_op jit(solution)/shard_map/write/pallas_call | solution.py:541
